TPU v7x, 32 devices: a whole 2x2x4 slice. The times are simulated.
32 devices in a mesh: rep: 2 (over x), y: 4 (over z), x: 4 (over y, core).
Axes of the slice: x: 2, y: 2, z: 4, core: 2. Of those that a mesh axis runs over, the one named last changes fastest.
Arguments:
- hidden: bfloat16 [64, 4096], P('rep', 'y'), parts along dimension 0
- lengths: int32 [64], P('rep'), parts along dimension 0
- k_cache: bfloat16 [2, 64, 128, 32, 128], P(None, ('rep', 'y'), None, 'x'), parts along dimension 1
- v_cache: bfloat16 [2, 64, 128, 32, 128], P(None, ('rep', 'y'), None, 'x'), parts along dimension 1
- rel_table: bfloat16 [2, 128, 32, 128], P(None, None, 'x')
- norm_attn: bfloat16 [2, 4096], P(None, 'y')
- w_q: bfloat16 [2, 4096, 32, 128], P(None, 'y', 'x')
- w_k: bfloat16 [2, 4096, 32, 128], P(None, 'y', 'x')
- w_v: bfloat16 [2, 4096, 32, 128], P(None, 'y', 'x')
- bias_content: bfloat16 [2, 32, 128], P(None, 'x')
- bias_pos: bfloat16 [2, 32, 128], P(None, 'x')
- w_out: bfloat16 [2, 32, 128, 4096], P(None, 'x', None, 'y')
- norm_mlp: bfloat16 [2, 4096], P(None, 'y')
- w_up: bfloat16 [2, 4096, 16384], P(None, 'y', 'x')
- w_down: bfloat16 [2, 16384, 4096], P(None, 'x', 'y')
Outputs:
- output 1: bfloat16 [64, 4096], P('rep', 'y'), parts along dimension 0
- output 2: bfloat16 [2, 64, 128, 32, 128], P(None, ('rep', 'y'), None, 'x'), parts along dimension 1
- output 3: bfloat16 [2, 64, 128, 32, 128], P(None, ('rep', 'y'), None, 'x'), parts along dimension 1
There are 2 independent parts. A program takes and returns all parts, laid end to end along the dimension named above; an argument that names none is the same for every part.
All inputs are finite; a program needn't handle non-finite values.
Results may differ from a plain program's by a relative error of at most 0.0197235.
Values are sent between devices in bfloat16 or wider.
A program may use at most 1 GiB of HBM per device.

v0:
```python
import jax
import jax.numpy as jnp
from jax import lax
from jax.sharding import PartitionSpec as P

EPS = 1e-6


def sharded_norm(hidden, gain, d_total):
    hidden_wide = hidden.astype(jnp.float32)
    sum_sq = lax.psum(jnp.sum(hidden_wide * hidden_wide, axis=1, keepdims=True), "y")
    inv_rms = lax.rsqrt(sum_sq / d_total + EPS)
    return (hidden_wide * inv_rms * gain.astype(jnp.float32)).astype(jnp.bfloat16)


def shift_rel(rel_all, lengths):
    seq_len = rel_all.shape[2]
    padded = jnp.pad(rel_all[:, :, ::-1], ((0, 0), (0, 0), (0, seq_len)))
    return jax.vmap(lambda rel_row, start_at: lax.dynamic_slice_in_dim(rel_row, start_at, seq_len, axis=1))(padded, seq_len - 1 - lengths)


def write_rows(cache_layer, new_rows, lengths):
    hit_mask = jnp.arange(cache_layer.shape[1])[None, :] == lengths[:, None]
    return jnp.where(hit_mask[:, :, None, None], new_rows[:, None, :, :], cache_layer)


def attend(q_rows, k_rows, v_rows, lengths, rel_layer, content_bias, pos_bias):
    q_wide = q_rows.astype(jnp.float32)
    q_content = (q_wide + content_bias.astype(jnp.float32)).astype(jnp.bfloat16)
    q_pos = (q_wide + pos_bias.astype(jnp.float32)).astype(jnp.bfloat16)
    scores = jnp.einsum("bhe,bshe->bhs", q_content, k_rows, preferred_element_type=jnp.float32)
    rel_all = jnp.einsum("bhe,the->bht", q_pos, rel_layer, preferred_element_type=jnp.float32)
    scores = (scores + shift_rel(rel_all, lengths)) * (q_rows.shape[2] ** -0.5)
    in_range = jnp.arange(k_rows.shape[1])[None, None, :] <= lengths[:, None, None]
    attn_prob = jax.nn.softmax(jnp.where(in_range, scores, -1e30), axis=-1).astype(jnp.bfloat16)
    return jnp.einsum("bhs,bshe->bhe", attn_prob, v_rows, preferred_element_type=jnp.float32).astype(jnp.bfloat16)


def solution(mesh):
    y_size = mesh.shape["y"]
    cache_spec = P(None, ("rep", "y"), None, "x", None)
    row_spec = P("rep", "y")
    proj_spec = P(None, "y", "x", None)
    head_spec = P(None, "x", None)
    in_specs = (row_spec, P("rep"), cache_spec, cache_spec, P(None, None, "x", None), P(None, "y"),
                proj_spec, proj_spec, proj_spec, head_spec, head_spec, P(None, "x", None, "y"),
                P(None, "y"), P(None, "y", "x"), P(None, "x", "y"))
    out_specs = (row_spec, cache_spec, cache_spec)

    def local_step(hidden, lengths, k_cache, v_cache, rel_table, norm_attn, w_q, w_k, w_v, bias_content, bias_pos, w_out, norm_mlp, w_up, w_down):
        rows_local = k_cache.shape[1]
        row_start = lax.axis_index("y") * rows_local
        len_local = lax.dynamic_slice_in_dim(lengths, row_start, rows_local)
        d_total = hidden.shape[1] * y_size
        k_layers = []
        v_layers = []
        for layer in range(k_cache.shape[0]):
            normed = sharded_norm(hidden, norm_attn[layer], d_total)
            q_part = jnp.einsum("bd,dhe->bhe", normed, w_q[layer], preferred_element_type=jnp.float32).astype(jnp.bfloat16)
            k_part = jnp.einsum("bd,dhe->bhe", normed, w_k[layer], preferred_element_type=jnp.float32).astype(jnp.bfloat16)
            v_part = jnp.einsum("bd,dhe->bhe", normed, w_v[layer], preferred_element_type=jnp.float32).astype(jnp.bfloat16)
            q_full, k_full, v_full = lax.psum((q_part, k_part, v_part), "y")
            q_rows = lax.dynamic_slice_in_dim(q_full, row_start, rows_local)
            k_rows = lax.dynamic_slice_in_dim(k_full, row_start, rows_local)
            v_rows = lax.dynamic_slice_in_dim(v_full, row_start, rows_local)
            k_new = write_rows(k_cache[layer], k_rows, len_local)
            v_new = write_rows(v_cache[layer], v_rows, len_local)
            k_layers.append(k_new)
            v_layers.append(v_new)
            context = attend(q_rows, k_new, v_new, len_local, rel_table[layer], bias_content[layer], bias_pos[layer])
            context_all = lax.all_gather(context, "y", axis=0, tiled=True)
            attn_part = jnp.einsum("bhe,hed->bd", context_all, w_out[layer], preferred_element_type=jnp.float32).astype(jnp.bfloat16)
            attn_out = lax.psum(attn_part, "x")
            hidden = (hidden.astype(jnp.float32) + attn_out.astype(jnp.float32)).astype(jnp.bfloat16)
            normed = sharded_norm(hidden, norm_mlp[layer], d_total)
            up_part = jnp.dot(normed, w_up[layer], preferred_element_type=jnp.float32).astype(jnp.bfloat16)
            up_proj = lax.psum(up_part, "y")
            activated = jax.nn.gelu(up_proj.astype(jnp.float32), approximate=True).astype(jnp.bfloat16)
            down_part = jnp.dot(activated, w_down[layer], preferred_element_type=jnp.float32).astype(jnp.bfloat16)
            down_out = lax.psum(down_part, "x")
            hidden = (hidden.astype(jnp.float32) + down_out.astype(jnp.float32)).astype(jnp.bfloat16)
        return hidden, jnp.stack(k_layers), jnp.stack(v_layers)

    return jax.shard_map(local_step, mesh=mesh, in_specs=in_specs, out_specs=out_specs, check_vma=False)
```

profile of v0, /device:TPU:0, one launch (start us, length us, event | category | flops | bytes accessed | tf_op | source)
XLA Modules:
  0.0 447.6 jit_solution(13353349327924337636)
XLA Ops:
  7.2 1.0 fusion.90
  8.2 13.5 %psum.112 = f32[32,1]{0,1:T(1,128)S(1)} all-reduce(f32[32,1]{0,1:T(1,128)S(1)} %bitcast.175), channel_id=1, replica_groups=mesh['rep'=2,'y'=4,'x'=4] {'y'}, use_global_device_ids=true, to_apply=%region_1.0 | all-reduce | flops 32 | bytes 256 | tf_op jit(solution)/shard_map/psum | solution.py:11
  22.5 2.6 fusion.153
  25.1 0.8 copy-done
  25.9 1.6 fusion.152
  27.5 1.1 fusion.54
  28.7 1.1 fusion.55
  29.8 1.6 fusion.151
  31.4 1.1 fusion.56
  33.0 33.1 %all-reduce.28.cloned.1.call-done = (bf16[32,8,128]{2,0,1:T(8,128)(2,1)}, bf16[32,8,128]{2,0,1:T(8,128)(2,1)}, bf16[32,8,128]{2,0,1:T(8,128)(2,1)}) async-done(((bf16[32,8,128]{2,0,1:T(8,128)(2,1)}, bf16[32,8,128]{2,0,1:T(8,128)(2,1)}, bf16[32,8,128]{2,0,1:T(8,128)(2,1)}), (bf16[32,8,128]{2,0,1:T(8,128)(2,1)}, bf16[32,8,128]{2,0,1:T(8,128)(2,1)}, ...) | async-done | bytes 196624 | tf_op jit(solution)/shard_map/psum | solution.py:62
  66.1 0.9 convolution_bitcast_fusion.1
  67.1 0.8 constant_dynamic-slice_fusion.1
  68.9 1.1 pad.8.clone
  69.9 2.0 gather_fusion
  71.9 15.6 %multiply_reduce_fusion.1 = f32[8,8,128]{1,2,0:T(8,128)S(1)} fusion(f32[8,8,128]{2,1,0:T(8,128)S(1)} %copy.85, pred[8,128]{1,0:T(8,128)(4,1)S(1)} %get-tuple-element.40, bf16[2,8,128,8,128]{4,3,2,1,0:T(8,128)(2,1)} %param.17, bf16[8,8,128]{2,1,0:T(8,128)(2,1)S(1)} %copy.41), kind=kLoop, calls=%fused_computation.19 | loop fusion | flops 4186112 | bytes 2180096
  88.4 4.9 %bitcast_select_fusion.2 = bf16[8,128,8,128]{3,2,1,0:T(8,128)(2,1)S(1)} fusion(pred[8,128]{1,0:T(8,128)(4,1)S(1)} %get-tuple-element.40, bf16[2,8,128,8,128]{4,3,2,1,0:T(8,128)(2,1)} %param.18, bf16[8,8,128]{2,1,0:T(8,128)(2,1)S(1)} %copy.45), kind=kLoop, calls=%fused_computation.39 | loop fusion | flops 1048576 | bytes 4211712 | tf_op jit(solution)/shard_map/jit(_where)/select_n | solution.py:24
  94.0 13.2 %all_gather.6 = bf16[32,8,128]{2,0,1:T(8,128)(2,1)S(1)} all-gather(bf16[8,8,128]{2,0,1:T(8,128)(2,1)S(1)} %bitcast.164), channel_id=1, replica_groups=mesh['rep'=2,'y'=4,'x'=4] {'y'}, dimensions={0}, use_global_device_ids=true | all-gather | bytes 81920 | tf_op jit(solution)/shard_map/all_gather | solution.py:71
  107.2 1.1 fusion.45
  108.4 31.3 %all-reduce.14.cloned.1.call-done = bf16[32,1024]{1,0:T(8,128)(2,1)} async-done(((bf16[32,1024]{1,0:T(8,128)(2,1)}), bf16[32,1024]{1,0:T(8,128)(2,1)}) %all-reduce.14.cloned.1.call-update) | async-done | bytes 65552 | tf_op jit(solution)/shard_map/psum | solution.py:73
  139.7 1.0 fusion.94
  140.7 11.7 %psum.117 = f32[32,1]{0,1:T(1,128)S(1)} all-reduce(f32[32,1]{0,1:T(1,128)S(1)} %bitcast.176), channel_id=1, replica_groups=mesh['rep'=2,'y'=4,'x'=4] {'y'}, use_global_device_ids=true, to_apply=%region_9.10 | all-reduce | flops 32 | bytes 256 | tf_op jit(solution)/shard_map/psum | solution.py:11
  152.4 5.7 %fusion.12 = bf16[32,4096]{1,0:T(8,128)(2,1)} fusion(bf16[2,1024,4096]{2,1,0:T(8,128)(2,1)} %param.28, f32[1024]{0:T(1024)S(1)} %bitcast.173, f32[32]{0:T(128)S(1)} %rsqrt_bitcast_fusion.2, bf16[32,1024]{1,0:T(8,128)(2,1)S(1)} %copy-done.3, bf16[32,1024]{1,0:T(8,128)(2,1)} %all-reduce.14.cloned.1.call-done), kind=kOutput, calls=%fused_computation.14 | convolution fusion | flops 268828672 | bytes 8786048 | tf_op jit(solution)/shard_map/dot_general | solution.py:76
  158.2 32.8 %all-reduce.16.cloned.1.call-done = bf16[32,4096]{1,0:T(8,128)(2,1)} async-done(((bf16[32,4096]{1,0:T(8,128)(2,1)}), bf16[32,4096]{1,0:T(8,128)(2,1)}) %all-reduce.16.cloned.1.call-update) | async-done | bytes 262160 | tf_op jit(solution)/shard_map/psum | solution.py:77
  190.9 5.6 %fusion.48 = bf16[32,1024]{1,0:T(8,128)(2,1)} fusion(bf16[2,4096,1024]{2,1,0:T(8,128)(2,1)} %param.29, bf16[32,4096]{1,0:T(8,128)(2,1)} %all-reduce.16.cloned.1.call-done), kind=kOutput, calls=%fused_computation.56 | convolution fusion | flops 269778944 | bytes 8716288 | tf_op jit(solution)/shard_map/dot_general | solution.py:79
  196.6 31.3 %all-reduce.18.cloned.1.call-done = bf16[32,1024]{1,0:T(8,128)(2,1)} async-done(((bf16[32,1024]{1,0:T(8,128)(2,1)}), bf16[32,1024]{1,0:T(8,128)(2,1)}) %all-reduce.18.cloned.1.call-update) | async-done | bytes 65552 | tf_op jit(solution)/shard_map/psum | solution.py:80
  228.0 1.0 fusion.98
  228.9 11.7 %psum.120 = f32[32,1]{0,1:T(1,128)S(1)} all-reduce(f32[32,1]{0,1:T(1,128)S(1)} %bitcast.174), channel_id=1, replica_groups=mesh['rep'=2,'y'=4,'x'=4] {'y'}, use_global_device_ids=true, to_apply=%region_13.14 | all-reduce | flops 32 | bytes 256 | tf_op jit(solution)/shard_map/psum | solution.py:11
  240.6 2.9 fusion.58
  243.5 1.1 fusion.59
  244.7 1.1 fusion.57
  246.1 32.3 %all-reduce.26.cloned.1.call-done = (bf16[32,8,128]{2,0,1:T(8,128)(2,1)}, bf16[32,8,128]{2,0,1:T(8,128)(2,1)}, bf16[32,8,128]{2,0,1:T(8,128)(2,1)}) async-done(((bf16[32,8,128]{2,0,1:T(8,128)(2,1)}, bf16[32,8,128]{2,0,1:T(8,128)(2,1)}, bf16[32,8,128]{2,0,1:T(8,128)(2,1)}), (bf16[32,8,128]{2,0,1:T(8,128)(2,1)}, bf16[32,8,128]{2,0,1:T(8,128)(2,1)}, ...) | async-done | bytes 196624 | tf_op jit(solution)/shard_map/psum | solution.py:62
  278.3 0.9 convolution_bitcast_fusion
  281.9 1.3 gather_fusion.1
  283.2 15.6 %multiply_reduce_fusion = f32[8,8,128]{1,2,0:T(8,128)S(1)} fusion(f32[8,8,128]{2,1,0:T(8,128)S(1)} %copy.86, pred[8,128]{1,0:T(8,128)(4,1)S(1)} %get-tuple-element.40, bf16[2,8,128,8,128]{4,3,2,1,0:T(8,128)(2,1)} %param.17, bf16[8,8,128]{2,1,0:T(8,128)(2,1)S(1)} %copy.48), kind=kLoop, calls=%fused_computation.18 | loop fusion | flops 4186112 | bytes 2180096
  299.7 4.9 %bitcast_select_fusion = bf16[8,128,8,128]{3,2,1,0:T(8,128)(2,1)S(1)} fusion(pred[8,128]{1,0:T(8,128)(4,1)S(1)} %get-tuple-element.40, bf16[2,8,128,8,128]{4,3,2,1,0:T(8,128)(2,1)} %param.18, bf16[8,8,128]{2,1,0:T(8,128)(2,1)S(1)} %copy.52), kind=kLoop, calls=%fused_computation.34 | loop fusion | flops 1048576 | bytes 4211712 | tf_op jit(solution)/shard_map/jit(_where)/select_n | solution.py:24
  305.3 13.2 %all_gather.7 = bf16[32,8,128]{2,0,1:T(8,128)(2,1)S(1)} all-gather(bf16[8,8,128]{2,0,1:T(8,128)(2,1)S(1)} %bitcast.165), channel_id=1, replica_groups=mesh['rep'=2,'y'=4,'x'=4] {'y'}, dimensions={0}, use_global_device_ids=true | all-gather | bytes 81920 | tf_op jit(solution)/shard_map/all_gather | solution.py:71
  318.5 1.1 fusion.42
  319.7 31.3 %all-reduce.20.cloned.1.call-done = bf16[32,1024]{1,0:T(8,128)(2,1)} async-done(((bf16[32,1024]{1,0:T(8,128)(2,1)}), bf16[32,1024]{1,0:T(8,128)(2,1)}) %all-reduce.20.cloned.1.call-update) | async-done | bytes 65552 | tf_op jit(solution)/shard_map/psum | solution.py:73
  351.0 1.0 fusion.102
  352.0 11.7 %psum.125 = f32[32,1]{0,1:T(1,128)S(1)} all-reduce(f32[32,1]{0,1:T(1,128)S(1)} %bitcast.177), channel_id=1, replica_groups=mesh['rep'=2,'y'=4,'x'=4] {'y'}, use_global_device_ids=true, to_apply=%region_21.22 | all-reduce | flops 32 | bytes 256 | tf_op jit(solution)/shard_map/psum | solution.py:11
  363.7 5.7 %fusion.15 = bf16[32,4096]{1,0:T(8,128)(2,1)} fusion(bf16[2,1024,4096]{2,1,0:T(8,128)(2,1)} %param.28, f32[1024]{0:T(1024)S(1)} %bitcast.169, f32[32]{0:T(128)S(1)} %rsqrt_bitcast_fusion, bf16[32,1024]{1,0:T(8,128)(2,1)S(1)} %get-tuple-element.12, bf16[32,1024]{1,0:T(8,128)(2,1)} %all-reduce.20.cloned.1.call-done), kind=kOutput, calls=%fused_computation.15 | convolution fusion | flops 268828672 | bytes 8786048 | tf_op jit(solution)/shard_map/dot_general | solution.py:76
  369.5 7.2 %broadcast_select_fusion.1 = (bf16[1,8,128,8,128]{4,3,2,1,0:T(8,128)(2,1)S(1)}, bf16[1,8,128,8,128]{4,3,2,1,0:T(8,128)(2,1)S(1)}, bf16[1,8,128,8,128]{4,3,2,1,0:T(8,128)(2,1)S(1)}, bf16[1,8,128,8,128]{4,3,2,1,0:T(8,128)(2,1)}) fusion(pred[8,128]{1,0:T(8,128)(4,1)S(1)} %get-tuple-element.40, bf16[2,8,128,8,128]{4,3,2,1,0:T(8,128)(2,1)} %param.18, ...), kind=kLoop, calls=%fused_computation.49 | loop fusion | flops 4194304 | bytes 16843776 | tf_op jit(solution)/shard_map/jit(_where)/select_n | solution.py:24
  376.6 2.4 pad_maximum_fusion.1
  379.0 23.2 %all-reduce.22.cloned.1.call-done = bf16[32,4096]{1,0:T(8,128)(2,1)} async-done(((bf16[32,4096]{1,0:T(8,128)(2,1)}), bf16[32,4096]{1,0:T(8,128)(2,1)}) %all-reduce.22.cloned.1.call-update) | async-done | bytes 262160 | tf_op jit(solution)/shard_map/psum | solution.py:77
  402.2 5.6 %fusion.51 = bf16[32,1024]{1,0:T(8,128)(2,1)} fusion(bf16[2,4096,1024]{2,1,0:T(8,128)(2,1)} %param.29, bf16[32,4096]{1,0:T(8,128)(2,1)} %all-reduce.22.cloned.1.call-done), kind=kOutput, calls=%fused_computation.57 | convolution fusion | flops 269778944 | bytes 8716288 | tf_op jit(solution)/shard_map/dot_general | solution.py:79
  407.9 4.0 pad_maximum_fusion
  411.9 27.3 %all-reduce.24.cloned.1.call-done = bf16[32,1024]{1,0:T(8,128)(2,1)} async-done(((bf16[32,1024]{1,0:T(8,128)(2,1)}), bf16[32,1024]{1,0:T(8,128)(2,1)}) %all-reduce.24.cloned.1.call-update) | async-done | bytes 65552 | tf_op jit(solution)/shard_map/psum | solution.py:80
  439.3 1.5 fusion.105
  (80 shorter events, 8.6 us)
Async XLA Ops:
  7.2 58.9 %all-reduce.28.cloned.1.call-start = ((), (), s32[]{:S(2)}) async-start(), calls=%async_computation.7 | async-start | bytes 393216 | tf_op jit(solution)/shard_map/psum | solution.py:62
  22.5 3.4 copy-start
  25.9 1.6 copy-start.3
  27.5 2.3 copy-start.1
  31.4 1.2 copy-start.10
  31.4 1.4 copy-start.8
  31.4 1.5 copy-start.4
  31.4 1.6 copy-start.9
  32.6 107.2 %all-reduce.14.cloned.1.call-start = ((), (), s32[]{:S(2)}) async-start(), calls=%async_computation | async-start | bytes 131072 | tf_op jit(solution)/shard_map/psum | solution.py:73
  88.4 18.8 %copy-start.11 = (bf16[2,8,128,1024]{3,2,1,0:T(8,128)(2,1)S(1)}, bf16[2,8,128,1024]{3,2,1,0:T(8,128)(2,1)}, u32[]{:S(2)}) copy-start(bf16[2,8,128,1024]{3,2,1,0:T(8,128)(2,1)} %param.26) | copy-start | bytes 12582916
  93.3 15.1 %copy-start.7 = (bf16[2,1024]{1,0:T(2,128)(2,1)S(1)}, bf16[2,1024]{1,0:T(2,128)(2,1)}, u32[]{:S(2)}) copy-start(bf16[2,1024]{1,0:T(2,128)(2,1)} %param.27) | copy-start | bytes 12292
  108.3 82.6 %all-reduce.16.cloned.1.call-start = ((), (), s32[]{:S(2)}) async-start(), calls=%async_computation.1 | async-start | bytes 524288 | tf_op jit(solution)/shard_map/psum | solution.py:77
  158.1 69.9 %copy-start.6 = (bf16[32,1024]{1,0:T(8,128)(2,1)S(1)}, bf16[32,1024]{1,0:T(8,128)(2,1)}, u32[]{:S(2)}) copy-start(bf16[32,1024]{1,0:T(8,128)(2,1)} %all-reduce.14.cloned.1.call-done) | copy-start | bytes 196612
  158.1 69.8 %all-reduce.18.cloned.1.call-start = ((), (), s32[]{:S(2)}) async-start(), calls=%async_computation.2 | async-start | bytes 131072 | tf_op jit(solution)/shard_map/psum | solution.py:80
  196.6 81.8 %all-reduce.26.cloned.1.call-start = ((), (), s32[]{:S(2)}) async-start(), calls=%async_computation.6 | async-start | bytes 393216 | tf_op jit(solution)/shard_map/psum | solution.py:62
  240.6 2.9 copy-start.2
  245.8 105.2 %all-reduce.20.cloned.1.call-start = ((), (), s32[]{:S(2)}) async-start(), calls=%async_computation.3 | async-start | bytes 131072 | tf_op jit(solution)/shard_map/psum | solution.py:73
  299.7 18.8 %copy-start.12 = (bf16[2,8,128,1024]{3,2,1,0:T(8,128)(2,1)S(1)}, bf16[2,8,128,1024]{3,2,1,0:T(8,128)(2,1)}, u32[]{:S(2)}) copy-start(bf16[2,8,128,1024]{3,2,1,0:T(8,128)(2,1)} %param.26) | copy-start | bytes 12582916
  319.6 82.6 %all-reduce.22.cloned.1.call-start = ((), (), s32[]{:S(2)}) async-start(), calls=%async_computation.4 | async-start | bytes 524288 | tf_op jit(solution)/shard_map/psum | solution.py:77
  369.4 69.9 %all-reduce.24.cloned.1.call-start = ((), (), s32[]{:S(2)}) async-start(), calls=%async_computation.5 | async-start | bytes 131072 | tf_op jit(solution)/shard_map/psum | solution.py:80
  407.9 31.4 %copy-start.5 = (bf16[32,1024]{1,0:T(8,128)(2,1)S(1)}, bf16[32,1024]{1,0:T(8,128)(2,1)}, u32[]{:S(2)}) copy-start(bf16[32,1024]{1,0:T(8,128)(2,1)} %all-reduce.20.cloned.1.call-done) | copy-start | bytes 196612
Sparse Core Ops, SparseCore 0:
  32.7 33.3 all-reduce.27
  108.4 31.2 all-reduce.13
  158.2 32.6 all-reduce.15
  196.7 31.2 all-reduce.17
  246.0 32.3 all-reduce.25
  319.8 31.2 all-reduce.19
  369.5 32.6 all-reduce.21
  408.0 31.2 all-reduce.23
where the time goes:
time: 449 us; the launch traced here: 448 us
  waiting for transfers between devices  243 us (54%)
  blocking collectives  75.1 us (17%)
  other arithmetic  63.6 us (14%)
  matrix products  36.6 us (8%)
  local copies, waits for them, and re-layouts  14.7 us (3%)
  between operations  14.4 us (3%)
    psum x2, waiting for transfers between devices, local_step(): q_full, k_full, v_full = lax.psum((q_part, k_part, v_part), 'y')  65.4 us
    psum x2, waiting for transfers between devices, local_step(): attn_out = lax.psum(attn_part, 'x')  62.6 us
    psum x2, waiting for transfers between devices, local_step(): down_out = lax.psum(down_part, 'x')  58.7 us
    psum x2, waiting for transfers between devices, local_step(): up_proj = lax.psum(up_part, 'y')  56 us
    psum x4, blocking collectives, sharded_norm(): lax.psum(jnp.sum(hidden_wide * hidden_wide, axis=1, keepdims=True), 'y')  48.6 us
    unnamed x4, other arithmetic  32.6 us
    all_gather x2, blocking collectives, local_step(): context_all = lax.all_gather(context, 'y', axis=0, tiled=True)  26.5 us
    select_n x3, other arithmetic, write_rows(): jnp.where(hit_mask[:, :, None, None], new_rows[:, None, :, :], cache_layer)  17 us
  transfers between devices with their start and end apart: 8, of which 8 were waited for; matrix products, arithmetic and copies ran while one was open for 3% of the time, Pallas kernels for 0%

commit v1 on v0

v1 whole, which is shorter than its diff:
```python
import functools

import jax
import jax.numpy as jnp
from jax import lax
from jax.experimental import pallas as pl
from jax.experimental.pallas import tpu as pltpu
from jax.sharding import PartitionSpec as P

EPS = 1e-6
MESH = pl.DeviceIdType.MESH
BF16 = jnp.bfloat16
F32 = jnp.float32
NT = (((1,), (1,)), ((), ()))


def dot(a, b):
    return jnp.dot(a, b, preferred_element_type=F32)


def layers_kernel(
    ny, nx,
    x_ref, len_ref, k_hbm, v_hbm, rel_hbm, ga_ref, wq_hbm, wk_hbm, wv_hbm, u_ref, w_ref, wo_hbm, gm_ref, wup_hbm, wdn_hbm,
    xout_ref, knew_ref, vnew_ref,
    wq, wk, wv, wo, wup, wdn, kbuf, vbuf, rel, relrev,
    xcur, hs, expand, acc, qkv_send, qkv_recv, stat, qkvf, ctxf, ctx_recv, lhs_wo, ar, up_send, up_recv, act,
    wsem, send_sem, recv_sem,
):
    layers = wup_hbm.shape[0]
    rows, dm = x_ref.shape
    rloc = rows // ny
    heads, hd = u_ref.shape[1:]
    ffc = wup.shape[3]
    seq = rel_hbm.shape[1]
    nblk = dm // 128
    r = lax.axis_index("rep")
    y = lax.axis_index("y")
    x = lax.axis_index("x")

    def loads(l):
        out = [
            (wq_hbm.at[l], wq.at[l]), (wk_hbm.at[l], wk.at[l]), (wv_hbm.at[l], wv.at[l]),
            (k_hbm.at[l], kbuf.at[l]), (rel_hbm.at[l], rel.at[l]), (v_hbm.at[l], vbuf.at[l]), (wo_hbm.at[l], wo.at[l]),
        ]
        for c in range(ny):
            out.append((wup_hbm.at[l, :, pl.ds(c * ffc, ffc)], wup.at[l, c]))
        for c in range(ny):
            out.append((wdn_hbm.at[l, pl.ds(c * ffc, ffc), :], wdn.at[l, c]))
        return [pltpu.make_async_copy(s, d, wsem.at[l, i]) for i, (s, d) in enumerate(out)]

    for l in range(layers):
        for c in loads(l):
            c.start()

    barrier = pltpu.get_barrier_semaphore()
    for d in range(1, ny):
        pl.semaphore_signal(barrier, inc=1, device_id=(r, lax.rem(y + d, ny), x), device_id_type=MESH)
    for d in range(1, nx):
        pl.semaphore_signal(barrier, inc=1, device_id=(r, y, lax.rem(x + d, nx)), device_id_type=MESH)

    xcur[...] = x_ref[...]
    e_row = lax.broadcasted_iota(jnp.int32, (128, 128 * heads), 0)
    e_col = lax.broadcasted_iota(jnp.int32, (128, 128 * heads), 1)
    expand[...] = jnp.where(e_col // heads == e_row, 1.0, 0.0).astype(BF16)

    pl.semaphore_wait(barrier, (ny - 1) + (nx - 1))

    def send(l, ph, src, dst, device, to):
        me, peer = to
        return pltpu.make_async_remote_copy(
            src_ref=src, dst_ref=dst, send_sem=send_sem.at[l, ph, peer], recv_sem=recv_sem.at[l, ph, me],
            device_id=device, device_id_type=MESH)

    def recv_wait(l, ph, buf, frm):
        pltpu.make_async_remote_copy(
            src_ref=buf, dst_ref=buf, send_sem=send_sem.at[l, ph, frm], recv_sem=recv_sem.at[l, ph, frm],
            device_id=(r, y, x), device_id_type=MESH).wait_recv()

    def send_wait(l, ph, buf, to):
        pltpu.make_async_remote_copy(
            src_ref=buf, dst_ref=buf, send_sem=send_sem.at[l, ph, to], recv_sem=recv_sem.at[l, ph, to],
            device_id=(r, y, x), device_id_type=MESH).wait_send()

    i32 = lax.broadcasted_iota(jnp.int32, (rows, 128), 0)
    l32 = lax.broadcasted_iota(jnp.int32, (rows, 128), 1)
    i8 = lax.broadcasted_iota(jnp.int32, (8, 128), 0)
    l8 = lax.broadcasted_iota(jnp.int32, (8, 128), 1)

    def gain_row(ref, l):
        g = ref[...].astype(F32)
        row = g[0:1]
        for i in range(1, layers):
            row = jnp.where(l == i, g[i:i + 1], row)
        return row

    def norm_local(l, ph, gain):
        xw = xcur[...].astype(F32)
        t = jnp.sum(xw * xw, axis=1, keepdims=True) * (1.0 / dm) + EPS
        t_row = jnp.sum(jnp.where(i32 == l32, jnp.broadcast_to(t, (rows, 128)), 0.0), axis=0, keepdims=True)
        stat[l, ph, y] = jnp.broadcast_to(t_row, (8, 128))
        for d in range(1, ny):
            py = lax.rem(y + d, ny)
            send(l, ph, stat.at[l, ph, y], stat.at[l, ph, y], (r, py, x), (y, py)).start()
        return (xw * lax.rsqrt(t) * gain).astype(BF16)

    def ratio_rows(l, ph):
        for d in range(1, ny):
            py = lax.rem(y + d, ny)
            recv_wait(l, ph, stat.at[l, ph, py], py)
        ts = [stat[l, ph, p] for p in range(ny)]
        mean = ts[0]
        for p in range(1, ny):
            mean = mean + ts[p]
        inv = lax.rsqrt(mean * (1.0 / ny))
        return [jnp.sqrt(t) * inv for t in ts]

    def all_reduce_x(l, ph, slot):
        for d in range(1, nx):
            px = lax.rem(x + d, nx)
            send(l, ph, ar.at[l, slot, x], ar.at[l, slot, x], (r, y, px), (x, px)).start()
        for d in range(1, nx):
            px = lax.rem(x + d, nx)
            recv_wait(l, ph, ar.at[l, slot, px], px)
        total = ar[l, slot, 0].astype(F32)
        for p in range(1, nx):
            total = total + ar[l, slot, p].astype(F32)
        xcur[...] = (xcur[...].astype(F32) + total).astype(BF16)

    def layer(l, carry):
        w = loads(l)
        h = norm_local(l, 0, gain_row(ga_ref, l))
        for b in range(nblk):
            hs[b] = h[:, b * 128:(b + 1) * 128]
        acc[...] = jnp.zeros_like(acc)
        w[0].wait()
        w[1].wait()
        w[2].wait()
        lane = lax.broadcasted_iota(jnp.int32, (rows, 128 * heads), 1) % heads

        def qkv_block(b, c):
            hx = dot(hs[b], expand[...])
            lhs = jnp.concatenate([jnp.where(lane == j, hx, 0.0) for j in range(heads)], axis=0).astype(BF16)
            ks = pl.ds(pl.multiple_of(b * 128 * heads, 128 * heads), 128 * heads)
            for i, wt in enumerate((wq, wk, wv)):
                acc[i] += dot(lhs, wt[l, ks, :])
            return c

        lax.fori_loop(0, nblk, qkv_block, 0)
        for p in range(ny):
            for i in range(3):
                a3 = acc[i].reshape(heads, rows, hd)
                qkv_send[p, i * heads:(i + 1) * heads] = a3[:, p * rloc:(p + 1) * rloc, :].astype(BF16)
        for d in range(1, ny):
            py = lax.rem(y + d, ny)
            send(l, 1, qkv_send.at[py], qkv_recv.at[l, y], (r, py, x), (y, py)).start()
        qkv_recv[l, y] = qkv_send[y]

        w[4].wait()

        def rev(t, c):
            relrev[seq - 1 - t] = rel[l, t]
            return c

        lax.fori_loop(0, seq, rev, 0)
        relrev[pl.ds(seq, seq)] = jnp.zeros((seq, heads, hd), BF16)

        ratios = ratio_rows(l, 0)
        cols = [jnp.sum(jnp.where(l8 == i8 + rloc * y, ra, 0.0), axis=1, keepdims=True) for ra in ratios]
        for d in range(1, ny):
            py = lax.rem(y + d, ny)
            recv_wait(l, 1, qkv_recv.at[l, py], py)
        tot = qkv_recv[l, 0].astype(F32) * cols[0][None]
        for p in range(1, ny):
            tot = tot + qkv_recv[l, p].astype(F32) * cols[p][None]
        qkvf[...] = tot.astype(BF16).astype(F32).reshape(3 * heads * rloc, hd)

        w[3].wait()
        w[5].wait()
        ul = u_ref[l].astype(F32)
        wl = w_ref[l].astype(F32)
        rel0 = relrev[seq - 1].astype(F32)
        sub = lax.broadcasted_iota(jnp.int32, (heads, seq * heads), 0)
        col = lax.broadcasted_iota(jnp.int32, (heads, seq * heads), 1)
        own = (col % heads) == sub
        pos = col // heads
        scale = hd ** -0.5

        def attend(b, c):
            length = len_ref[rloc * y + b]
            q = qkvf[pl.ds(b, heads, stride=rloc), :]
            k = qkvf[pl.ds(heads * rloc + b, heads, stride=rloc), :]
            v = qkvf[pl.ds(2 * heads * rloc + b, heads, stride=rloc), :]
            knew_ref[l, b] = k.astype(BF16)
            vnew_ref[l, b] = v.astype(BF16)
            a = (q + ul).astype(BF16)
            cc = (q + wl).astype(BF16)
            window = relrev[pl.ds(seq - 1 - length, seq)].reshape(seq * heads, hd)
            s = lax.dot_general(a, kbuf[l, b], NT, preferred_element_type=F32)
            s = s + lax.dot_general(cc, window, NT, preferred_element_type=F32)
            s = jnp.where(own & (pos < length), s * scale, -1e30)
            sn = jnp.sum(a.astype(F32) * k + cc.astype(F32) * rel0, axis=1, keepdims=True) * scale
            m = jnp.maximum(jnp.max(s, axis=1, keepdims=True), sn)
            e = jnp.exp(s - m)
            en = jnp.exp(sn - m)
            z = jnp.sum(e, axis=1, keepdims=True) + en
            pr = (e / z).astype(BF16)
            pn = (en / z).astype(BF16).astype(F32)
            ctx = dot(pr, vbuf[l, b]) + pn * v
            ctxf[pl.ds(pl.multiple_of(b * heads, heads), heads), :] = ctx
            return c

        for b in range(rloc):
            attend(b, 0)
        for j in range(heads):
            ctx_recv[l, y, j] = ctxf[pl.ds(j, rloc, stride=heads), :].astype(BF16)
        for d in range(1, ny):
            py = lax.rem(y + d, ny)
            send(l, 2, ctx_recv.at[l, y], ctx_recv.at[l, y], (r, py, x), (y, py)).start()
        for d in range(1, ny):
            py = lax.rem(y + d, ny)
            recv_wait(l, 2, ctx_recv.at[l, py], py)

        for j in range(heads):
            lhs_wo[:, j * hd:(j + 1) * hd] = jnp.concatenate(
                [ctx_recv[l, p, j].astype(F32) for p in range(ny)], axis=0).astype(BF16)
        w[6].wait()
        ar[l, 0, x] = dot(lhs_wo[...], wo[l]).astype(BF16)
        all_reduce_x(l, 3, 0)

        h2 = norm_local(l, 4, gain_row(gm_ref, l))
        for i in range(ny):
            w[7 + i].wait()
        hs_flat = h2

        for d in range(1, ny + 1):
            py = lax.rem(y + d, ny)
            part = dot(hs_flat, wup[l, py]).astype(BF16)
            if d < ny:
                up_send[py] = part
                send(l, 5, up_send.at[py], up_recv.at[l, y], (r, py, x), (y, py)).start()
            else:
                up_recv[l, y] = part
        ratios = ratio_rows(l, 4)
        cols = [jnp.sum(jnp.where(l32 == i32, ra[0:1], 0.0), axis=1, keepdims=True) for ra in ratios]
        for d in range(1, ny):
            py = lax.rem(y + d, ny)
            recv_wait(l, 5, up_recv.at[l, py], py)
        up = up_recv[l, 0].astype(F32) * cols[0]
        for p in range(1, ny):
            up = up + up_recv[l, p].astype(F32) * cols[p]
        up = up.astype(BF16).astype(F32)
        act[l, y] = jax.nn.gelu(up, approximate=True).astype(BF16)
        for d in range(1, ny):
            py = lax.rem(y + d, ny)
            send(l, 6, act.at[l, y], act.at[l, y], (r, py, x), (y, py)).start()
        for i in range(ny):
            w[7 + ny + i].wait()
        down = dot(act[l, y], wdn[l, y])
        for d in range(1, ny):
            py = lax.rem(y + d, ny)
            recv_wait(l, 6, act.at[l, py], py)
            down = down + dot(act[l, py], wdn[l, py])
        ar[l, 1, x] = down.astype(BF16)
        all_reduce_x(l, 7, 1)
        for d in range(1, ny):
            py = lax.rem(y + d, ny)
            send_wait(l, 1, qkv_send.at[py], py)
            send_wait(l, 5, up_send.at[py], py)
        return carry

    lax.fori_loop(0, layers, layer, 0)
    xout_ref[...] = xcur[...]

    def drain(l, carry):
        for d in range(1, ny):
            py = lax.rem(y + d, ny)
            send_wait(l, 0, stat.at[l, 0, y], py)
            send_wait(l, 2, ctx_recv.at[l, y], py)
            send_wait(l, 4, stat.at[l, 4, y], py)
            send_wait(l, 6, act.at[l, y], py)
        for d in range(1, nx):
            px = lax.rem(x + d, nx)
            send_wait(l, 3, ar.at[l, 0, x], px)
            send_wait(l, 7, ar.at[l, 1, x], px)
        return carry

    lax.fori_loop(0, layers, drain, 0)


def write_rows(cache, new_rows, lengths):
    hit = jnp.arange(cache.shape[2])[None, None, :] == lengths[None, :, None]
    return jnp.where(hit[:, :, :, None, None], new_rows[:, :, None, :, :], cache)


def solution(mesh):
    ny, nx = mesh.shape["y"], mesh.shape["x"]
    cache_spec = P(None, ("rep", "y"), None, "x", None)
    row_spec = P("rep", "y")
    proj_spec = P(None, "y", "x", None)
    head_spec = P(None, "x", None)
    in_specs = (row_spec, P("rep"), cache_spec, cache_spec, P(None, None, "x", None), P(None, "y"),
                proj_spec, proj_spec, proj_spec, head_spec, head_spec, P(None, "x", None, "y"),
                P(None, "y"), P(None, "y", "x"), P(None, "x", "y"))
    out_specs = (row_spec, cache_spec, cache_spec)

    def local_step(hidden, lengths, k_cache, v_cache, rel_table, norm_attn, w_q, w_k, w_v, bias_content, bias_pos, w_out, norm_mlp, w_up, w_down):
        rows, dm = hidden.shape
        layers, rloc, seq, heads, hd = k_cache.shape
        ff = w_up.shape[2]
        ffc = ff // ny
        flat = (layers, dm * heads, hd)
        vm = pl.BlockSpec(memory_space=pltpu.VMEM)
        sm = pl.BlockSpec(memory_space=pltpu.SMEM)
        hbm = pl.BlockSpec(memory_space=pl.ANY)
        new_shape = jax.ShapeDtypeStruct((layers, rloc, heads, hd), BF16)
        nph = 8
        npeer = max(ny, nx)
        out, k_new, v_new = pl.pallas_call(
            functools.partial(layers_kernel, ny, nx),
            name="decode_layers",
            out_shape=(jax.ShapeDtypeStruct((rows, dm), BF16), new_shape, new_shape),
            in_specs=[vm, sm, hbm, hbm, hbm, vm, hbm, hbm, hbm, vm, vm, hbm, vm, hbm, hbm],
            out_specs=(vm, vm, vm),
            scratch_shapes=[
                pltpu.VMEM(flat, BF16), pltpu.VMEM(flat, BF16), pltpu.VMEM(flat, BF16),
                pltpu.VMEM((layers, heads * hd, dm), BF16),
                pltpu.VMEM((layers, ny, dm, ffc), BF16),
                pltpu.VMEM((layers, ny, ffc, dm), BF16),
                pltpu.VMEM((layers, rloc, seq * heads, hd), BF16),
                pltpu.VMEM((layers, rloc, seq * heads, hd), BF16),
                pltpu.VMEM((layers, seq, heads, hd), BF16),
                pltpu.VMEM((2 * seq, heads, hd), BF16),
                pltpu.VMEM((rows, dm), BF16),
                pltpu.VMEM((dm // 128, rows, 128), BF16),
                pltpu.VMEM((128, 128 * heads), BF16),
                pltpu.VMEM((3, heads * rows, hd), F32),
                pltpu.VMEM((ny, 3 * heads, rloc, hd), BF16),
                pltpu.VMEM((layers, ny, 3 * heads, rloc, hd), BF16),
                pltpu.VMEM((layers, nph, ny, 8, 128), F32),
                pltpu.VMEM((3 * heads * rloc, hd), F32),
                pltpu.VMEM((rloc * heads, hd), F32),
                pltpu.VMEM((layers, ny, heads, rloc, hd), BF16),
                pltpu.VMEM((rows, heads * hd), BF16),
                pltpu.VMEM((layers, 2, nx, rows, dm), BF16),
                pltpu.VMEM((ny, rows, ffc), BF16),
                pltpu.VMEM((layers, ny, rows, ffc), BF16),
                pltpu.VMEM((layers, ny, rows, ffc), BF16),
                pltpu.SemaphoreType.DMA((layers, 7 + 2 * ny)),
                pltpu.SemaphoreType.DMA((layers, nph, npeer)),
                pltpu.SemaphoreType.DMA((layers, nph, npeer)),
            ],
            compiler_params=pltpu.CompilerParams(
                collective_id=0, has_side_effects=True, vmem_limit_bytes=67043328),
        )(hidden, lengths, k_cache.reshape(layers, rloc, seq * heads, hd), v_cache.reshape(layers, rloc, seq * heads, hd),
          rel_table, norm_attn, w_q.reshape(flat), w_k.reshape(flat), w_v.reshape(flat), bias_content, bias_pos,
          w_out.reshape(layers, heads * hd, dm), norm_mlp, w_up, w_down)
        row_start = lax.axis_index("y") * rloc
        len_local = lax.dynamic_slice_in_dim(lengths, row_start, rloc)
        return out, write_rows(k_cache, k_new, len_local), write_rows(v_cache, v_new, len_local)

    return jax.shard_map(local_step, mesh=mesh, in_specs=in_specs, out_specs=out_specs, check_vma=False)
```

time: 449 us -> 105 us (0.23)
  waiting for transfers between devices: 243 us -> 0 us
  Pallas kernels: 0 us -> 94.1 us
  blocking collectives: 75.1 us -> 0 us
  other arithmetic: 63.6 us -> 8.1 us
  matrix products: 36.6 us -> 0 us
  between operations: 14.4 us -> 0.65 us
  local copies, waits for them, and re-layouts: 14.7 us -> 1.37 us
    psum x8 -> x0, waiting for transfers between devices: 243 us -> none  [the longest x2 65.4 us: local_step(): q_full, k_full, v_full = lax.psum((q_part, k_part, v_part), 'y')]
    pallas_call x0 -> x1, Pallas kernels: none -> 94.1 us  [local_step(): pl.pallas_call(functools.partial(layers_kernel, ny, nx), name='decode_lay...]
    psum x4 -> x0, blocking collectives: 48.6 us -> none  [sharded_norm(): lax.psum(jnp.sum(hidden_wide * hidden_wide, axis=1, keepdims=True), 'y')]
    dot_general x16 -> x0, matrix products: 36.6 us -> none  [the longest x2 11.4 us: local_step(): jnp.dot(normed, w_up[layer], preferred_element_type=jnp.float32)]
    unnamed x4 -> x0, other arithmetic: 32.6 us -> none
    all_gather x2 -> x0, blocking collectives: 26.5 us -> none  [local_step(): context_all = lax.all_gather(context, 'y', axis=0, tiled=True)]
    select_n x3 -> x1, other arithmetic: 17 us -> 7.46 us  [write_rows(): jnp.where(hit[:, :, :, None, None], new_rows[:, :, None, :, :], cache)]
    another operation x2 -> x0, other arithmetic: 6.39 us -> none  [local_step(): return (hidden, jnp.stack(k_layers), jnp.stack(v_layers))]
  transfers between devices with their start and end apart: 8 -> 0, of which waited for: 8 -> 0; matrix products, arithmetic and copies ran while one was open for 3% -> 0% of each run, Pallas kernels for 0% -> 0%
where the time goes in v1:
time: 105 us; the launch traced here: 104 us
  Pallas kernels  94.1 us (90%)
  other arithmetic  8.1 us (8%)
  local copies, waits for them, and re-layouts  1.37 us (1%)
    pallas_call x1, Pallas kernels, local_step(): pl.pallas_call(functools.partial(layers_kernel, ny, nx), name='decode_lay...  94.1 us
    select_n x1, other arithmetic, write_rows(): jnp.where(hit[:, :, :, None, None], new_rows[:, :, None, :, :], cache)  7.46 us

profile of v1, /device:TPU:0, one launch (start us, length us, event | category | flops | bytes accessed | tf_op | source)
XLA Modules:
  0.0 104.2 jit_solution(5551495396267182150)
XLA Ops:
  0.6 0.7 dynamic_slice.3
  1.4 0.6 iota_compare_fusion
  2.0 94.1 %decode_layers.1 = (bf16[32,1024]{1,0:T(8,128)(2,1)}, bf16[2,8,8,128]{3,2,1,0:T(8,128)(2,1)}, bf16[2,8,8,128]{3,2,1,0:T(8,128)(2,1)}) custom-call(bf16[32,1024]{1,0:T(8,128)(2,1)} %x_ref.1, s32[32]{0:T(128)} %len_ref.1, bf16[2,8,1024,128]{3,2,1,0:T(8,128)(2,1)} %bitcast.6, bf16[2,8,1024,128]{3,2,1,0:T(8,128)(2,1)} %bitcast.7, ...), custom_call_target="tpu_custom_call" | custom-call | tf_op jit(solution)/shard_map/decode_layers/pallas_call | solution.py:318
  96.1 0.0 copy-start
  96.1 7.5 %broadcast_select_fusion = (bf16[2,8,128,8,128]{4,3,2,1,0:T(8,128)(2,1)}, bf16[2,8,128,8,128]{4,3,2,1,0:T(8,128)(2,1)}) fusion(bf16[2,8,128,8,128]{4,3,2,1,0:T(8,128)(2,1)} %param.18, pred[8,128]{1,0:T(8,128)(4,1)} %iota_compare_fusion, bf16[2,8,8,128]{3,2,1,0:T(8,128)(2,1)} %get-tuple-element.8, bf16[2,8,128,8,128]{4,3,2,1,0:T(8,128)(2,1)} %param.17, ...), kind=kLoop, calls=%fused_computation | loop fusion | flops 4194304 | bytes 16843776 | tf_op jit(solution)/shard_map/jit(_where)/select_n | solution.py:292
  103.5 0.0 copy-done
  103.5 0.6 copy.19
Async XLA Ops:
  96.1 7.5 %copy-start = (bf16[32,1024]{1,0:T(8,128)(2,1)S(1)}, bf16[32,1024]{1,0:T(8,128)(2,1)}, u32[]{:S(2)}) copy-start(bf16[32,1024]{1,0:T(8,128)(2,1)} %get-tuple-element.14) | copy-start | bytes 196612

commit v2 on v1

v2 whole, which is shorter than its diff:
```python
import functools

import jax
import jax.numpy as jnp
from jax import lax
from jax.experimental import pallas as pl
from jax.experimental.pallas import tpu as pltpu
from jax.sharding import PartitionSpec as P

EPS = 1e-6
MESH = pl.DeviceIdType.MESH
BF16 = jnp.bfloat16
F32 = jnp.float32
NT = (((1,), (1,)), ((), ()))


def dot(a, b):
    return jnp.dot(a, b, preferred_element_type=F32)


def layers_kernel(
    ny, nx, nch,
    x_ref, len_ref, k_hbm, v_hbm, rel_hbm, ga_ref, wq_hbm, wk_hbm, wv_hbm, u_ref, w_ref, wo_hbm, gm_ref, wup_hbm, wdn_hbm,
    xout_ref, knew_ref, vnew_ref,
    wq, wk, wv, wo, wup, wdn, kbuf, vbuf, rel, relrev,
    xcur, hs, expand, lhs, qkv_send, qkv_recv, stat, qkvf, scores, ctxf, ctx_recv, lhs_wo, ar, up_send, up_recv, act, down,
    wsem, send_sem, recv_sem,
):
    layers = wup_hbm.shape[0]
    rows, dm = x_ref.shape
    rloc = rows // ny
    heads, hd = u_ref.shape[1:]
    ffc = wup.shape[3]
    sub_ff = ffc // nch
    seq = rel_hbm.shape[1]
    nblk = dm // 128
    wide = 128 * heads
    r = lax.axis_index("rep")
    y = lax.axis_index("y")
    x = lax.axis_index("x")
    half = y // 2
    ypeers = [3 - 3 * half, 2 - half, 1 - y + 4 * half] if ny == 4 else [lax.rem(y + d, ny) for d in range(1, ny)]
    xpeers = [lax.rem(x + 2, nx), 3 - x, x + 1 - 2 * lax.rem(x, 2)] if nx == 4 else [lax.rem(x + d, nx) for d in range(1, nx)]

    def load_qkv(l):
        pairs = [(wq_hbm.at[l], wq), (wk_hbm.at[l], wk), (wv_hbm.at[l], wv)]
        return [pltpu.make_async_copy(s, d, wsem.at[l, i]) for i, (s, d) in enumerate(pairs)]

    def load_rest(l):
        out = [(k_hbm.at[l], kbuf.at[l]), (rel_hbm.at[l], rel.at[l]), (v_hbm.at[l], vbuf.at[l]), (wo_hbm.at[l], wo.at[l])]
        for c in range(ny):
            out.append((wup_hbm.at[l, :, pl.ds(c * ffc, ffc)], wup.at[l, c]))
        for c in range(ny):
            out.append((wdn_hbm.at[l, pl.ds(c * ffc, ffc), :], wdn.at[l, c]))
        return [pltpu.make_async_copy(s, d, wsem.at[l, 3 + i]) for i, (s, d) in enumerate(out)]

    for c in load_qkv(0):
        c.start()
    for l in range(layers):
        for c in load_rest(l):
            c.start()

    barrier = pltpu.get_barrier_semaphore()
    for py in ypeers:
        pl.semaphore_signal(barrier, inc=1, device_id=(r, py, x), device_id_type=MESH)
    for px in xpeers:
        pl.semaphore_signal(barrier, inc=1, device_id=(r, y, px), device_id_type=MESH)

    xcur[...] = x_ref[...]
    e_row = lax.broadcasted_iota(jnp.int32, (128, wide), 0)
    e_col = lax.broadcasted_iota(jnp.int32, (128, wide), 1)
    expand[...] = jnp.where(e_col // heads == e_row, 1.0, 0.0).astype(BF16)
    i32 = lax.broadcasted_iota(jnp.int32, (rows, 128), 0)
    l32 = lax.broadcasted_iota(jnp.int32, (rows, 128), 1)
    i8 = lax.broadcasted_iota(jnp.int32, (8, 128), 0)
    l8 = lax.broadcasted_iota(jnp.int32, (8, 128), 1)

    pl.semaphore_wait(barrier, (ny - 1) + (nx - 1))

    def copy_y(l, ph, src, dst, py):
        return pltpu.make_async_remote_copy(
            src_ref=src, dst_ref=dst, send_sem=send_sem.at[l, ph, py], recv_sem=recv_sem.at[l, ph, y],
            device_id=(r, py, x), device_id_type=MESH)

    def copy_x(l, ph, src, dst, px):
        return pltpu.make_async_remote_copy(
            src_ref=src, dst_ref=dst, send_sem=send_sem.at[l, ph, px], recv_sem=recv_sem.at[l, ph, x],
            device_id=(r, y, px), device_id_type=MESH)

    def local(l, ph, buf, i):
        return pltpu.make_async_remote_copy(
            src_ref=buf, dst_ref=buf, send_sem=send_sem.at[l, ph, i], recv_sem=recv_sem.at[l, ph, i],
            device_id=(r, y, x), device_id_type=MESH)

    def gain_row(ref, l):
        g = ref[...].astype(F32)
        row = g[0:1]
        for i in range(1, layers):
            row = jnp.where(l == i, g[i:i + 1], row)
        return row

    def norm_local(l, ph, gain):
        xw = xcur[...].astype(F32)
        t = jnp.sum(xw * xw, axis=1, keepdims=True) * (1.0 / dm) + EPS
        t_row = jnp.sum(jnp.where(i32 == l32, jnp.broadcast_to(t, (rows, 128)), 0.0), axis=0, keepdims=True)
        stat[l, ph, y] = jnp.broadcast_to(t_row, (8, 128))
        for py in ypeers:
            copy_y(l, ph, stat.at[l, ph, y], stat.at[l, ph, y], py).start()
        return (xw * lax.rsqrt(t) * gain).astype(BF16)

    def ratio_rows(l, ph):
        for py in ypeers:
            local(l, ph, stat.at[l, ph, py], py).wait_recv()
        ts = [stat[l, ph, p] for p in range(ny)]
        mean = ts[0]
        for p in range(1, ny):
            mean = mean + ts[p]
        inv = lax.rsqrt(mean * (1.0 / ny))
        return [jnp.sqrt(t) * inv for t in ts]

    def all_reduce_x(l, ph, slot):
        for px in xpeers:
            copy_x(l, ph, ar.at[l, slot, x], ar.at[l, slot, x], px).start()
        for px in xpeers:
            local(l, ph, ar.at[l, slot, px], px).wait_recv()
        total = ar[l, slot, 0].astype(F32)
        for p in range(1, nx):
            total = total + ar[l, slot, p].astype(F32)
        xcur[...] = (xcur[...].astype(F32) + total).astype(BF16)

    PQ, PC, PA, PD, PU, PG = 2, 5, 6, 7, 8, 8 + nch

    def layer(l, carry):
        wl_qkv = load_qkv(l)
        wl = load_rest(l)
        h = norm_local(l, 0, gain_row(ga_ref, l))
        for b in range(nblk):
            hs[b * rows:(b + 1) * rows, :] = h[:, b * 128:(b + 1) * 128]
        lane = lax.broadcasted_iota(jnp.int32, (rows, wide), 1) % heads
        for b in range(nblk):
            hx = dot(hs[b * rows:(b + 1) * rows, :], expand[...])
            if b >= nblk // 2:
                hx = -hx
            for j in range(heads):
                lhs[j * rows:(j + 1) * rows, b * wide:(b + 1) * wide] = jnp.where(lane == j, hx, 0.0).astype(BF16)

        def scatter(i, part):
            a3 = part.reshape(heads, rows, hd)
            for p in range(ny):
                qkv_send[i, p] = a3[:, p * rloc:(p + 1) * rloc, :].astype(BF16)
            for py in ypeers:
                copy_y(l, PQ + i, qkv_send.at[i, py], qkv_recv.at[l, i, y], py).start()
            qkv_recv[l, i, y] = qkv_send[i, y]

        wl_qkv[0].wait()
        wl_qkv[1].wait()
        kh = dm * heads // 2
        qk = (dot(lhs[:, :kh], jnp.concatenate([wq[:kh, :], wk[:kh, :]], axis=1))
              - dot(lhs[:, kh:], jnp.concatenate([wq[kh:, :], wk[kh:, :]], axis=1)))
        scatter(0, qk[:, :hd])
        scatter(1, qk[:, hd:])
        wl_qkv[2].wait()
        scatter(2, dot(lhs[:, :kh], wv[:kh, :]) - dot(lhs[:, kh:], wv[kh:, :]))

        @pl.when(l + 1 < layers)
        def _():
            for c in load_qkv(l + 1):
                c.start()

        wl[1].wait()

        def rev(t, c):
            relrev[seq - 1 - t] = rel[l, t]
            return c

        lax.fori_loop(0, seq, rev, 0, unroll=8)
        relrev[pl.ds(seq, seq)] = jnp.zeros((seq, heads, hd), BF16)

        ratios = ratio_rows(l, 0)
        cols = [jnp.sum(jnp.where(l8 == i8 + rloc * y, ra, 0.0), axis=1, keepdims=True) for ra in ratios]

        def gather(i):
            for py in ypeers:
                local(l, PQ + i, qkv_recv.at[l, i, py], py).wait_recv()
            tot = qkv_recv[l, i, 0].astype(F32) * cols[0][None]
            for p in range(1, ny):
                tot = tot + qkv_recv[l, i, p].astype(F32) * cols[p][None]
            qkvf[i] = tot.astype(BF16).astype(F32).reshape(heads * rloc, hd)

        wl[0].wait()
        gather(0)
        ul = u_ref[l].astype(F32)
        wl_pos = w_ref[l].astype(F32)
        rel0 = relrev[seq - 1].astype(F32)
        sub = lax.broadcasted_iota(jnp.int32, (heads, seq * heads), 0)
        col = lax.broadcasted_iota(jnp.int32, (heads, seq * heads), 1)
        own = (col % heads) == sub
        pos = col // heads
        scale = hd ** -0.5

        def query(b):
            q = qkvf[0, pl.ds(b, heads, stride=rloc), :]
            return (q + ul).astype(BF16), (q + wl_pos).astype(BF16)

        for b in range(rloc):
            length = len_ref[rloc * y + b]
            a, cc = query(b)
            window = relrev[pl.ds(seq - 1 - length, seq)].reshape(seq * heads, hd)
            s = lax.dot_general(a, kbuf[l, b], NT, preferred_element_type=F32)
            s = s + lax.dot_general(cc, window, NT, preferred_element_type=F32)
            scores[b] = jnp.where(own & (pos < length), s * scale, -1e30)
        gather(1)
        wl[2].wait()
        gather(2)
        for b in range(rloc):
            a, cc = query(b)
            k = qkvf[1, pl.ds(b, heads, stride=rloc), :]
            v = qkvf[2, pl.ds(b, heads, stride=rloc), :]
            knew_ref[l, b] = k.astype(BF16)
            vnew_ref[l, b] = v.astype(BF16)
            s = scores[b]
            sn = jnp.sum(a.astype(F32) * k + cc.astype(F32) * rel0, axis=1, keepdims=True) * scale
            m = jnp.maximum(jnp.max(s, axis=1, keepdims=True), sn)
            e = jnp.exp(s - m)
            en = jnp.exp(sn - m)
            z = jnp.sum(e, axis=1, keepdims=True) + en
            pr = (e / z).astype(BF16)
            pn = (en / z).astype(BF16).astype(F32)
            ctxf[b * heads:(b + 1) * heads, :] = dot(pr, vbuf[l, b]) + pn * v
        for j in range(heads):
            ctx_recv[l, y, j] = ctxf[pl.ds(j, rloc, stride=heads), :].astype(BF16)
        for py in ypeers:
            copy_y(l, PC, ctx_recv.at[l, y], ctx_recv.at[l, y], py).start()
        for py in ypeers:
            local(l, PC, ctx_recv.at[l, py], py).wait_recv()

        for j in range(heads):
            lhs_wo[:, j * hd:(j + 1) * hd] = jnp.concatenate(
                [ctx_recv[l, p, j].astype(F32) for p in range(ny)], axis=0).astype(BF16)
        wl[3].wait()
        ar[l, 0, x] = dot(lhs_wo[...], wo[l]).astype(BF16)
        all_reduce_x(l, PA, 0)

        h2 = norm_local(l, 1, gain_row(gm_ref, l))
        for i in range(ny):
            wl[4 + i].wait()
        for ch in range(nch):
            cs = slice(ch * sub_ff, (ch + 1) * sub_ff)
            for py in ypeers:
                up_send[py, ch] = dot(h2, wup[l, py, :, cs]).astype(BF16)
                copy_y(l, PU + ch, up_send.at[py, ch], up_recv.at[l, y, ch], py).start()
            up_recv[l, y, ch] = dot(h2, wup[l, y, :, cs]).astype(BF16)
        ratios = ratio_rows(l, 1)
        cols2 = [jnp.sum(jnp.where(l32 == i32, ra[0:1], 0.0), axis=1, keepdims=True) for ra in ratios]
        for i in range(ny):
            wl[4 + ny + i].wait()
        for ch in range(nch):
            for py in ypeers:
                local(l, PU + ch, up_recv.at[l, py, ch], py).wait_recv()
            up = up_recv[l, 0, ch].astype(F32) * cols2[0]
            for p in range(1, ny):
                up = up + up_recv[l, p, ch].astype(F32) * cols2[p]
            up = up.astype(BF16).astype(F32)
            act[l, y, ch] = jax.nn.gelu(up, approximate=True).astype(BF16)
            for py in ypeers:
                copy_y(l, PG + ch, act.at[l, y, ch], act.at[l, y, ch], py).start()
            part = dot(act[l, y, ch], wdn[l, y, ch * sub_ff:(ch + 1) * sub_ff, :])
            if ch == 0:
                down[...] = part
            else:
                down[...] += part
        for ch in range(nch):
            for py in ypeers[::-1]:
                local(l, PG + ch, act.at[l, py, ch], py).wait_recv()
                down[...] += dot(act[l, py, ch], wdn[l, py, ch * sub_ff:(ch + 1) * sub_ff, :])
        ar[l, 1, x] = down[...].astype(BF16)
        all_reduce_x(l, PD, 1)
        for py in ypeers:
            for i in range(3):
                local(l, PQ + i, qkv_send.at[i, py], py).wait_send()
            for ch in range(nch):
                local(l, PU + ch, up_send.at[py, ch], py).wait_send()
        return carry

    lax.fori_loop(0, layers, layer, 0)
    xout_ref[...] = xcur[...]

    def drain(l, carry):
        for py in ypeers:
            local(l, 0, stat.at[l, 0, y], py).wait_send()
            local(l, 1, stat.at[l, 1, y], py).wait_send()
            local(l, PC, ctx_recv.at[l, y], py).wait_send()
            for ch in range(nch):
                local(l, PG + ch, act.at[l, y, ch], py).wait_send()
        for px in xpeers:
            local(l, PA, ar.at[l, 0, x], px).wait_send()
            local(l, PD, ar.at[l, 1, x], px).wait_send()
        return carry

    lax.fori_loop(0, layers, drain, 0)


def write_kernel(x_ref, len_ref, kn_ref, vn_ref, k_hbm, v_hbm, xout_ref, kout, vout, buf, in_sem, out_sem):
    layers, rloc = kn_ref.shape[:2]
    y = lax.axis_index("y")
    units = [(s, n, o, l) for l in range(layers) for s, n, o in ((k_hbm, kn_ref, kout), (v_hbm, vn_ref, vout))]
    nsplit = 2
    per = rloc // nsplit
    steps = [(s, n, o, l, q) for (s, n, o, l) in units for q in range(nsplit)]
    ins = [pltpu.make_async_copy(s.at[l, q * per:(q + 1) * per], buf.at[i], in_sem.at[i]) for i, (s, n, o, l, q) in enumerate(steps)]
    outs = [pltpu.make_async_copy(buf.at[i], o.at[l, q * per:(q + 1) * per], out_sem.at[i]) for i, (s, n, o, l, q) in enumerate(steps)]
    for c in ins:
        c.start()
    xout_ref[...] = x_ref[...]
    for i, (s, n, o, l, q) in enumerate(steps):
        ins[i].wait()
        for b in range(per):
            buf[i, b, len_ref[rloc * y + q * per + b]] = n[l, q * per + b]
        outs[i].start()
    for c in outs:
        c.wait()


def solution(mesh):
    ny, nx = mesh.shape["y"], mesh.shape["x"]
    cache_spec = P(None, ("rep", "y"), None, "x", None)
    row_spec = P("rep", "y")
    proj_spec = P(None, "y", "x", None)
    head_spec = P(None, "x", None)
    in_specs = (row_spec, P("rep"), cache_spec, cache_spec, P(None, None, "x", None), P(None, "y"),
                proj_spec, proj_spec, proj_spec, head_spec, head_spec, P(None, "x", None, "y"),
                P(None, "y"), P(None, "y", "x"), P(None, "x", "y"))
    out_specs = (row_spec, cache_spec, cache_spec)

    def local_step(hidden, lengths, k_cache, v_cache, rel_table, norm_attn, w_q, w_k, w_v, bias_content, bias_pos, w_out, norm_mlp, w_up, w_down):
        rows, dm = hidden.shape
        layers, rloc, seq, heads, hd = k_cache.shape
        ff = w_up.shape[2]
        ffc = ff // ny
        flat = (layers, dm * heads, hd)
        vm = pl.BlockSpec(memory_space=pltpu.VMEM)
        sm = pl.BlockSpec(memory_space=pltpu.SMEM)
        hbm = pl.BlockSpec(memory_space=pl.ANY)
        new_shape = jax.ShapeDtypeStruct((layers, rloc, heads, hd), BF16)
        nch = 2
        sub_ff = ffc // nch
        nph = 8 + 2 * nch
        npeer = max(ny, nx)
        out, k_new, v_new = pl.pallas_call(
            functools.partial(layers_kernel, ny, nx, nch),
            name="decode_layers",
            out_shape=(jax.ShapeDtypeStruct((rows, dm), BF16), new_shape, new_shape),
            in_specs=[vm, sm, hbm, hbm, hbm, vm, hbm, hbm, hbm, vm, vm, hbm, vm, hbm, hbm],
            out_specs=(vm, vm, vm),
            scratch_shapes=[
                pltpu.VMEM(flat[1:], BF16), pltpu.VMEM(flat[1:], BF16), pltpu.VMEM(flat[1:], BF16),
                pltpu.VMEM((layers, heads * hd, dm), BF16),
                pltpu.VMEM((layers, ny, dm, ffc), BF16),
                pltpu.VMEM((layers, ny, ffc, dm), BF16),
                pltpu.VMEM((layers, rloc, seq * heads, hd), BF16),
                pltpu.VMEM((layers, rloc, seq * heads, hd), BF16),
                pltpu.VMEM((layers, seq, heads, hd), BF16),
                pltpu.VMEM((2 * seq, heads, hd), BF16),
                pltpu.VMEM((rows, dm), BF16),
                pltpu.VMEM((dm // 128 * rows, 128), BF16),
                pltpu.VMEM((128, 128 * heads), BF16),
                pltpu.VMEM((heads * rows, dm * heads), BF16),
                pltpu.VMEM((3, ny, heads, rloc, hd), BF16),
                pltpu.VMEM((layers, 3, ny, heads, rloc, hd), BF16),
                pltpu.VMEM((layers, 2, ny, 8, 128), F32),
                pltpu.VMEM((3, heads * rloc, hd), F32),
                pltpu.VMEM((rloc, heads, seq * heads), F32),
                pltpu.VMEM((rloc * heads, hd), F32),
                pltpu.VMEM((layers, ny, heads, rloc, hd), BF16),
                pltpu.VMEM((rows, heads * hd), BF16),
                pltpu.VMEM((layers, 2, nx, rows, dm), BF16),
                pltpu.VMEM((ny, nch, rows, sub_ff), BF16),
                pltpu.VMEM((layers, ny, nch, rows, sub_ff), BF16),
                pltpu.VMEM((layers, ny, nch, rows, sub_ff), BF16),
                pltpu.VMEM((rows, dm), F32),
                pltpu.SemaphoreType.DMA((layers, 7 + 2 * ny)),
                pltpu.SemaphoreType.DMA((layers, nph, npeer)),
                pltpu.SemaphoreType.DMA((layers, nph, npeer)),
            ],
            compiler_params=pltpu.CompilerParams(
                collective_id=0, has_side_effects=True, vmem_limit_bytes=67043328),
        )(hidden, lengths, k_cache.reshape(layers, rloc, seq * heads, hd), v_cache.reshape(layers, rloc, seq * heads, hd),
          rel_table, norm_attn, w_q.reshape(flat), w_k.reshape(flat), w_v.reshape(flat), bias_content, bias_pos,
          w_out.reshape(layers, heads * hd, dm), norm_mlp, w_up, w_down)
        nunit = 2 * layers * 2
        cache_shape = jax.ShapeDtypeStruct(k_cache.shape, BF16)
        return pl.pallas_call(
            write_kernel,
            name="write_caches",
            out_shape=(jax.ShapeDtypeStruct((rows, dm), BF16), cache_shape, cache_shape),
            in_specs=[vm, sm, vm, vm, hbm, hbm],
            out_specs=(vm, hbm, hbm),
            scratch_shapes=[
                pltpu.VMEM((nunit, rloc // 2, seq, heads, hd), BF16),
                pltpu.SemaphoreType.DMA((nunit,)),
                pltpu.SemaphoreType.DMA((nunit,)),
            ],
            compiler_params=pltpu.CompilerParams(vmem_limit_bytes=16 << 20),
        )(out, lengths, k_new, v_new, k_cache, v_cache)

    return jax.shard_map(local_step, mesh=mesh, in_specs=in_specs, out_specs=out_specs, check_vma=False)
```

time: 105 us -> 91.5 us (0.87)
  Pallas kernels: 94.1 us -> 83 us
  other arithmetic: 8.1 us -> 0 us
  local copies, waits for them, and re-layouts: 1.37 us -> 7.38 us
    pallas_call x1 -> x2, Pallas kernels: 94.1 us -> 83 us  [the longest x1 77.8 us: local_step(): pl.pallas_call(functools.partial(layers_kernel, ny, nx, nch), name='decod...]
    select_n x1 -> x0, other arithmetic: 7.46 us -> none  [write_rows(): jnp.where(hit[:, :, :, None, None], new_rows[:, :, None, :, :], cache)]
    unnamed x3 -> x12, local copies, waits for them, and re-layouts: 0.63 us -> 7.38 us
where the time goes in v2:
time: 91.5 us; the launch traced here: 91.1 us
  Pallas kernels  83 us (91%)
  local copies, waits for them, and re-layouts  7.38 us (8%)
    pallas_call x1, Pallas kernels, local_step(): pl.pallas_call(functools.partial(layers_kernel, ny, nx, nch), name='decod...  77.8 us
    unnamed x12, local copies, waits for them, and re-layouts  7.38 us
    pallas_call x1, Pallas kernels, local_step(): pl.pallas_call(write_kernel, name='write_caches', out_shape=(jax.ShapeDty...  5.19 us

profile of v2, /device:TPU:0, one launch (start us, length us, event | category | flops | bytes accessed | tf_op | source)
XLA Modules:
  0.0 91.1 jit_solution(11104374961273923839)
XLA Ops:
  0.6 77.8 %decode_layers.1 = (bf16[32,1024]{1,0:T(8,128)(2,1)}, bf16[2,8,8,128]{3,2,1,0:T(8,128)(2,1)}, bf16[2,8,8,128]{3,2,1,0:T(8,128)(2,1)}) custom-call(bf16[32,1024]{1,0:T(8,128)(2,1)} %x_ref.1, s32[32]{0:T(128)} %len_ref.3, bf16[2,8,1024,128]{3,2,1,0:T(8,128)(2,1)} %bitcast.6, bf16[2,8,1024,128]{3,2,1,0:T(8,128)(2,1)} %bitcast.7, ...), custom_call_target="tpu_custom_call" | custom-call | tf_op jit(solution)/shard_map/decode_layers/pallas_call | solution.py:349
  78.5 0.0 copy-start
  78.5 2.2 %copy-done = bf16[2,8,128,8,128]{4,3,2,1,0:T(8,128)(2,1)S(1)} copy-done((bf16[2,8,128,8,128]{4,3,2,1,0:T(8,128)(2,1)S(1)}, bf16[2,8,128,8,128]{4,3,2,1,0:T(8,128)(2,1)}, u32[]{:S(2)}) %copy-start) | copy-done | bytes 4194328
  80.7 0.0 copy-start.1
  80.7 2.2 %copy-done.1 = bf16[2,8,128,8,128]{4,3,2,1,0:T(8,128)(2,1)S(1)} copy-done((bf16[2,8,128,8,128]{4,3,2,1,0:T(8,128)(2,1)S(1)}, bf16[2,8,128,8,128]{4,3,2,1,0:T(8,128)(2,1)}, u32[]{:S(2)}) %copy-start.1) | copy-done | bytes 4194328
  82.9 0.0 copy-start.2
  82.9 0.8 copy-done.2
  83.7 0.0 copy-start.3
  83.7 0.8 copy-done.3
  84.5 0.0 copy-start.4
  84.5 0.8 copy-done.4
  85.2 0.0 copy-start.5
  85.2 0.7 copy-done.5
  85.9 5.2 %write_caches.1 = (bf16[32,1024]{1,0:T(8,128)(2,1)}, bf16[2,8,128,8,128]{4,3,2,1,0:T(8,128)(2,1)}, bf16[2,8,128,8,128]{4,3,2,1,0:T(8,128)(2,1)}) custom-call(bf16[32,1024]{1,0:T(8,128)(2,1)S(1)} %copy-done.2, s32[32]{0:T(128)S(1)} %copy-done.5, bf16[2,8,8,128]{3,2,1,0:T(8,128)(2,1)S(1)} %copy-done.3, bf16[2,8,8,128]{3,2,1,0:T(8,128)(2,1)S(1)} %copy-done.4, ...), custom_call_target="tpu_custom_call" | custom-call | tf_op jit(solution)/shard_map/write_caches/pallas_call | solution.py:392
Async XLA Ops:
  78.5 2.2 %copy-start = (bf16[2,8,128,8,128]{4,3,2,1,0:T(8,128)(2,1)S(1)}, bf16[2,8,128,8,128]{4,3,2,1,0:T(8,128)(2,1)}, u32[]{:S(2)}) copy-start(bf16[2,8,128,8,128]{4,3,2,1,0:T(8,128)(2,1)} %k_hbm.1) | copy-start | bytes 12582916
  80.7 2.2 %copy-start.1 = (bf16[2,8,128,8,128]{4,3,2,1,0:T(8,128)(2,1)S(1)}, bf16[2,8,128,8,128]{4,3,2,1,0:T(8,128)(2,1)}, u32[]{:S(2)}) copy-start(bf16[2,8,128,8,128]{4,3,2,1,0:T(8,128)(2,1)} %v_hbm.1) | copy-start | bytes 12582916
  82.9 0.8 copy-start.2
  83.7 0.8 copy-start.3
  84.5 0.8 copy-start.4
  85.2 0.7 copy-start.5

commit v3 on v2

v3 whole, which is shorter than its diff:
```python
import functools

import jax
import jax.numpy as jnp
from jax import lax
from jax.experimental import pallas as pl
from jax.experimental.pallas import tpu as pltpu
from jax.sharding import PartitionSpec as P

EPS = 1e-6
MESH = pl.DeviceIdType.MESH
BF16 = jnp.bfloat16
F32 = jnp.float32
NT = (((1,), (1,)), ((), ()))


def dot(a, b):
    return jnp.dot(a, b, preferred_element_type=F32)


def layers_kernel(
    ny, nx, ns,
    x_ref, len_ref, k_hbm, v_hbm, rel_hbm, ga_ref, wq_hbm, wk_hbm, wv_hbm, u_ref, w_ref, wo_hbm, gm_ref, wup_hbm, wdn_hbm,
    xout_ref, knew_ref, vnew_ref,
    wq, wk, wv, wo, wup, wdn, kbuf, vbuf, rel, relrev,
    xcur, hrep, expand, lhs, qkv_send, qkv_recv, stat, qkvf, ctxf, ctx_recv, lhs_wo, ar, up_send, up_recv, act, down,
    wsem, send_sem, recv_sem,
):
    layers = wup_hbm.shape[0]
    rows, dm = x_ref.shape
    rloc = rows // ny
    srow = rows // ns
    sloc = rloc // ns
    heads, hd = u_ref.shape[1:]
    ffc = wup.shape[3]
    seq = rel_hbm.shape[1]
    nblk = dm // 128
    wide = 128 * heads
    grp = heads * sloc
    r = lax.axis_index("rep")
    y = lax.axis_index("y")
    x = lax.axis_index("x")
    half = y // 2
    ypeers = [3 - 3 * half, 2 - half, 1 - y + 4 * half] if ny == 4 else [lax.rem(y + d, ny) for d in range(1, ny)]
    xpeers = [lax.rem(x + 2, nx), 3 - x, x + 1 - 2 * lax.rem(x, 2)] if nx == 4 else [lax.rem(x + d, nx) for d in range(1, nx)]

    def load_qkv(l):
        pairs = [(wq_hbm.at[l], wq), (wk_hbm.at[l], wk), (wv_hbm.at[l], wv)]
        return [pltpu.make_async_copy(s, d, wsem.at[l, i]) for i, (s, d) in enumerate(pairs)]

    def load_rest(l):
        out = [(k_hbm.at[l], kbuf.at[l]), (rel_hbm.at[l], rel.at[l]), (v_hbm.at[l], vbuf.at[l]), (wo_hbm.at[l], wo.at[l])]
        for c in range(ny):
            out.append((wup_hbm.at[l, :, pl.ds(c * ffc, ffc)], wup.at[l, c]))
        for c in range(ny):
            out.append((wdn_hbm.at[l, pl.ds(c * ffc, ffc), :], wdn.at[l, c]))
        return [pltpu.make_async_copy(s, d, wsem.at[l, 3 + i]) for i, (s, d) in enumerate(out)]

    for c in load_qkv(0):
        c.start()
    for l in range(layers):
        for c in load_rest(l):
            c.start()

    barrier = pltpu.get_barrier_semaphore()
    for py in ypeers:
        pl.semaphore_signal(barrier, inc=1, device_id=(r, py, x), device_id_type=MESH)
    for px in xpeers:
        pl.semaphore_signal(barrier, inc=1, device_id=(r, y, px), device_id_type=MESH)

    def iota(shape, dim):
        return lax.broadcasted_iota(jnp.int32, shape, dim)

    def ones_where(mask):
        return jnp.where(mask, 1.0, 0.0).astype(BF16)

    expand[...] = ones_where(iota((128, wide), 1) // heads == iota((128, wide), 0))

    def pick(s, shape, dim):
        j = iota(shape, dim)
        return (j // sloc) * rloc + s * sloc + j % sloc == iota(shape, 1 - dim)

    for s in range(ns):
        xcur[s] = dot(ones_where(pick(s, (srow, rows), 0)), x_ref[...]).astype(BF16)
    mi = iota((ny * grp, srow), 0)
    repeat = ones_where((mi // grp) * sloc + mi % sloc == iota((ny * grp, srow), 1))
    own_head = (iota((ny * grp, wide), 0) // sloc) % heads == iota((ny * grp, wide), 1) % heads
    irow = iota((srow, 128), 0)
    lrow = iota((srow, 128), 1)
    igrp = iota((grp, 128), 0) % sloc + sloc * y
    lgrp = iota((grp, 128), 1)

    pl.semaphore_wait(barrier, (ny - 1) + (nx - 1))

    def copy_y(l, s, ph, src, dst, py):
        return pltpu.make_async_remote_copy(
            src_ref=src, dst_ref=dst, send_sem=send_sem.at[l, s, ph, py], recv_sem=recv_sem.at[l, s, ph, y],
            device_id=(r, py, x), device_id_type=MESH)

    def copy_x(l, s, ph, src, dst, px):
        return pltpu.make_async_remote_copy(
            src_ref=src, dst_ref=dst, send_sem=send_sem.at[l, s, ph, px], recv_sem=recv_sem.at[l, s, ph, x],
            device_id=(r, y, px), device_id_type=MESH)

    def local(l, s, ph, buf, i):
        return pltpu.make_async_remote_copy(
            src_ref=buf, dst_ref=buf, send_sem=send_sem.at[l, s, ph, i], recv_sem=recv_sem.at[l, s, ph, i],
            device_id=(r, y, x), device_id_type=MESH)

    def gain_row(ref, l):
        g = ref[...].astype(F32)
        row = g[0:1]
        for i in range(1, layers):
            row = jnp.where(l == i, g[i:i + 1], row)
        return row

    def norm_local(l, s, ph, gain):
        xw = xcur[s].astype(F32)
        t = jnp.sum(xw * xw, axis=1, keepdims=True) * (1.0 / dm) + EPS
        t_row = jnp.sum(jnp.where(irow == lrow, jnp.broadcast_to(t, (srow, 128)), 0.0), axis=0, keepdims=True)
        stat[l, s, ph, y] = jnp.broadcast_to(t_row, (8, 128))
        for py in ypeers:
            copy_y(l, s, ph, stat.at[l, s, ph, y], stat.at[l, s, ph, y], py).start()
        return (xw * lax.rsqrt(t) * gain).astype(BF16)

    def ratio_rows(l, s, ph):
        for py in ypeers:
            local(l, s, ph, stat.at[l, s, ph, py], py).wait_recv()
        ts = [stat[l, s, ph, p][0:1] for p in range(ny)]
        mean = ts[0]
        for p in range(1, ny):
            mean = mean + ts[p]
        inv = lax.rsqrt(mean * (1.0 / ny))
        return [jnp.sqrt(t) * inv for t in ts]

    def reduce_start(l, s, ph, slot):
        for px in xpeers:
            copy_x(l, s, ph, ar.at[l, s, slot, x], ar.at[l, s, slot, x], px).start()

    def reduce_finish(l, s, ph, slot):
        for px in xpeers:
            local(l, s, ph, ar.at[l, s, slot, px], px).wait_recv()
        total = ar[l, s, slot, 0].astype(F32)
        for p in range(1, nx):
            total = total + ar[l, s, slot, p].astype(F32)
        xcur[s] = (xcur[s].astype(F32) + total).astype(BF16)

    PQ, PC, PA, PD, PU, PG = 2, 5, 6, 7, 8, 9

    def project(l, s, first):
        wl = load_qkv(l)
        h = norm_local(l, s, 0, gain_row(ga_ref, l))
        hrep[...] = dot(repeat, h).astype(BF16)
        for b in range(nblk):
            hx = dot(hrep[:, b * 128:(b + 1) * 128], expand[...])
            lhs[:, b * wide:(b + 1) * wide] = jnp.where(own_head, hx if b < nblk // 2 else -hx, 0.0).astype(BF16)
        kh = dm * heads // 2

        def scatter(i, part):
            for p in range(ny):
                qkv_send[s, i, p] = part[p * grp:(p + 1) * grp, :].astype(BF16)
            for py in ypeers:
                copy_y(l, s, PQ + i, qkv_send.at[s, i, py], qkv_recv.at[l, s, i, y], py).start()
            qkv_recv[l, s, i, y] = qkv_send[s, i, y]

        if first:
            wl[0].wait()
            wl[1].wait()
        qk = (dot(lhs[:, :kh], jnp.concatenate([wq[:kh, :], wk[:kh, :]], axis=1))
              - dot(lhs[:, kh:], jnp.concatenate([wq[kh:, :], wk[kh:, :]], axis=1)))
        scatter(0, qk[:, :hd])
        scatter(1, qk[:, hd:])
        if first:
            wl[2].wait()
        scatter(2, dot(lhs[:, :kh], wv[:kh, :]) - dot(lhs[:, kh:], wv[kh:, :]))

    sub = iota((heads, seq * heads), 0)
    col = iota((heads, seq * heads), 1)
    scale = hd ** -0.5

    def attend(l, s, first):
        wl = load_rest(l)
        own = (col % heads) == sub
        pos = col // heads
        ratios = ratio_rows(l, s, 0)
        cols = [jnp.sum(jnp.where(lgrp == igrp, ra, 0.0), axis=1, keepdims=True) for ra in ratios]

        def gather(i):
            for py in ypeers:
                local(l, s, PQ + i, qkv_recv.at[l, s, i, py], py).wait_recv()
            tot = qkv_recv[l, s, i, 0].astype(F32) * cols[0]
            for p in range(1, ny):
                tot = tot + qkv_recv[l, s, i, p].astype(F32) * cols[p]
            qkvf[i] = tot.astype(BF16).astype(F32)

        if first:
            wl[0].wait()
        gather(0)
        ul = u_ref[l].astype(F32)
        pl_bias = w_ref[l].astype(F32)
        rel0 = relrev[seq - 1].astype(F32)
        queries = []
        scores = []
        for b in range(sloc):
            length = len_ref[rloc * y + s * sloc + b]
            q = qkvf[0, pl.ds(b, heads, stride=sloc), :]
            a, cc = (q + ul).astype(BF16), (q + pl_bias).astype(BF16)
            queries.append((a, cc))
            window = relrev[pl.ds(seq - 1 - length, seq)].reshape(seq * heads, hd)
            sc = lax.dot_general(a, kbuf[l, s * sloc + b], NT, preferred_element_type=F32)
            sc = sc + lax.dot_general(cc, window, NT, preferred_element_type=F32)
            scores.append(jnp.where(own & (pos < length), sc * scale, -1e30))
        gather(1)
        if first:
            wl[2].wait()
        gather(2)
        for b in range(sloc):
            a, cc = queries[b]
            sc = scores[b]
            k = qkvf[1, pl.ds(b, heads, stride=sloc), :]
            v = qkvf[2, pl.ds(b, heads, stride=sloc), :]
            knew_ref[l, s * sloc + b] = k.astype(BF16)
            vnew_ref[l, s * sloc + b] = v.astype(BF16)
            sn = jnp.sum(a.astype(F32) * k + cc.astype(F32) * rel0, axis=1, keepdims=True) * scale
            m = jnp.maximum(jnp.max(sc, axis=1, keepdims=True), sn)
            e = jnp.exp(sc - m)
            en = jnp.exp(sn - m)
            z = jnp.sum(e, axis=1, keepdims=True) + en
            pr = (e / z).astype(BF16)
            pn = (en / z).astype(BF16).astype(F32)
            ctxf[b * heads:(b + 1) * heads, :] = dot(pr, vbuf[l, s * sloc + b]) + pn * v
        ctx_recv[l, s, y] = ctxf[0:grp, :].astype(BF16)
        for py in ypeers:
            copy_y(l, s, PC, ctx_recv.at[l, s, y], ctx_recv.at[l, s, y], py).start()

    def project_out(l, s, first):
        for py in ypeers:
            local(l, s, PC, ctx_recv.at[l, s, py], py).wait_recv()
        for p in range(ny):
            ctxf[p * grp:(p + 1) * grp, :] = ctx_recv[l, s, p].astype(F32)
        for j in range(heads):
            lhs_wo[:, j * hd:(j + 1) * hd] = ctxf[pl.ds(j, srow, stride=heads), :].astype(BF16)
        if first:
            load_rest(l)[3].wait()
        ar[l, s, 0, x] = dot(lhs_wo[...], wo[l]).astype(BF16)
        reduce_start(l, s, PA, 0)

    def ff_up(l, s, first):
        reduce_finish(l, s, PA, 0)
        h2 = norm_local(l, s, 1, gain_row(gm_ref, l))
        if first:
            for c in load_rest(l)[4:4 + ny]:
                c.wait()
        for py in ypeers:
            up_send[s, py] = dot(h2, wup[l, py]).astype(BF16)
            copy_y(l, s, PU, up_send.at[s, py], up_recv.at[l, s, y], py).start()
        up_recv[l, s, y] = dot(h2, wup[l, y]).astype(BF16)

    def ff_act(l, s, first):
        ratios = ratio_rows(l, s, 1)
        cols = [jnp.sum(jnp.where(lrow == irow, ra, 0.0), axis=1, keepdims=True) for ra in ratios]
        for py in ypeers:
            local(l, s, PU, up_recv.at[l, s, py], py).wait_recv()
        up = up_recv[l, s, 0].astype(F32) * cols[0]
        for p in range(1, ny):
            up = up + up_recv[l, s, p].astype(F32) * cols[p]
        up = up.astype(BF16).astype(F32)
        act[l, s, y] = jax.nn.gelu(up, approximate=True).astype(BF16)
        for py in ypeers:
            copy_y(l, s, PG, act.at[l, s, y], act.at[l, s, y], py).start()
        if first:
            for c in load_rest(l)[4 + ny:]:
                c.wait()
        down[s] = dot(act[l, s, y], wdn[l, y])

    def ff_down(l, s, first):
        for py in ypeers[::-1]:
            local(l, s, PG, act.at[l, s, py], py).wait_recv()
            down[s] += dot(act[l, s, py], wdn[l, py])
        ar[l, s, 1, x] = down[s].astype(BF16)
        reduce_start(l, s, PD, 1)

    def reverse_rel(l):
        load_rest(l)[1].wait()

        def rev(t, c):
            relrev[seq - 1 - t] = rel[l, t]
            return c

        lax.fori_loop(0, seq, rev, 0, unroll=8)

    relrev[pl.ds(seq, seq)] = jnp.zeros((seq, heads, hd), BF16)

    def layer(l, carry):
        for s in range(ns):
            @pl.when(l > 0)
            def _():
                reduce_finish(l - 1, s, PD, 1)

            project(l, s, s == 0)

        @pl.when(l + 1 < layers)
        def _():
            for c in load_qkv(l + 1):
                c.start()

        reverse_rel(l)
        for stage in (attend, project_out, ff_up, ff_act, ff_down):
            for s in range(ns):
                stage(l, s, s == 0)
        for s in range(ns):
            for py in ypeers:
                for i in range(3):
                    local(l, s, PQ + i, qkv_send.at[s, i, py], py).wait_send()
                local(l, s, PU, up_send.at[s, py], py).wait_send()
        return carry

    lax.fori_loop(0, layers, layer, 0)
    total = None
    for s in range(ns):
        reduce_finish(layers - 1, s, PD, 1)
        part = dot(ones_where(pick(s, (rows, srow), 1)), xcur[s])
        total = part if total is None else total + part
    xout_ref[...] = total.astype(BF16)

    def drain(l, carry):
        for s in range(ns):
            for py in ypeers:
                local(l, s, 0, stat.at[l, s, 0, y], py).wait_send()
                local(l, s, 1, stat.at[l, s, 1, y], py).wait_send()
                local(l, s, PC, ctx_recv.at[l, s, y], py).wait_send()
                local(l, s, PG, act.at[l, s, y], py).wait_send()
            for px in xpeers:
                local(l, s, PA, ar.at[l, s, 0, x], px).wait_send()
                local(l, s, PD, ar.at[l, s, 1, x], px).wait_send()
        return carry

    lax.fori_loop(0, layers, drain, 0)


def write_kernel(x_ref, len_ref, kn_ref, vn_ref, k_hbm, v_hbm, xout_ref, kout, vout, buf, in_sem, out_sem):
    layers, rloc = kn_ref.shape[:2]
    y = lax.axis_index("y")
    units = [(s, n, o, l) for l in range(layers) for s, n, o in ((k_hbm, kn_ref, kout), (v_hbm, vn_ref, vout))]
    nsplit = 2
    per = rloc // nsplit
    steps = [(s, n, o, l, q) for (s, n, o, l) in units for q in range(nsplit)]
    ins = [pltpu.make_async_copy(s.at[l, q * per:(q + 1) * per], buf.at[i], in_sem.at[i]) for i, (s, n, o, l, q) in enumerate(steps)]
    outs = [pltpu.make_async_copy(buf.at[i], o.at[l, q * per:(q + 1) * per], out_sem.at[i]) for i, (s, n, o, l, q) in enumerate(steps)]
    for c in ins:
        c.start()
    xout_ref[...] = x_ref[...]
    for i, (s, n, o, l, q) in enumerate(steps):
        ins[i].wait()
        for b in range(per):
            buf[i, b, len_ref[rloc * y + q * per + b]] = n[l, q * per + b]
        outs[i].start()
    for c in outs:
        c.wait()


def solution(mesh):
    ny, nx = mesh.shape["y"], mesh.shape["x"]
    cache_spec = P(None, ("rep", "y"), None, "x", None)
    row_spec = P("rep", "y")
    proj_spec = P(None, "y", "x", None)
    head_spec = P(None, "x", None)
    in_specs = (row_spec, P("rep"), cache_spec, cache_spec, P(None, None, "x", None), P(None, "y"),
                proj_spec, proj_spec, proj_spec, head_spec, head_spec, P(None, "x", None, "y"),
                P(None, "y"), P(None, "y", "x"), P(None, "x", "y"))
    out_specs = (row_spec, cache_spec, cache_spec)

    def local_step(hidden, lengths, k_cache, v_cache, rel_table, norm_attn, w_q, w_k, w_v, bias_content, bias_pos, w_out, norm_mlp, w_up, w_down):
        rows, dm = hidden.shape
        layers, rloc, seq, heads, hd = k_cache.shape
        ff = w_up.shape[2]
        ffc = ff // ny
        flat = (layers, dm * heads, hd)
        vm = pl.BlockSpec(memory_space=pltpu.VMEM)
        sm = pl.BlockSpec(memory_space=pltpu.SMEM)
        hbm = pl.BlockSpec(memory_space=pl.ANY)
        new_shape = jax.ShapeDtypeStruct((layers, rloc, heads, hd), BF16)
        ns = 2
        srow = rows // ns
        grp = heads * (rloc // ns)
        nph = 10
        npeer = max(ny, nx)
        out, k_new, v_new = pl.pallas_call(
            functools.partial(layers_kernel, ny, nx, ns),
            name="decode_layers",
            out_shape=(jax.ShapeDtypeStruct((rows, dm), BF16), new_shape, new_shape),
            in_specs=[vm, sm, hbm, hbm, hbm, vm, hbm, hbm, hbm, vm, vm, hbm, vm, hbm, hbm],
            out_specs=(vm, vm, vm),
            scratch_shapes=[
                pltpu.VMEM(flat[1:], BF16), pltpu.VMEM(flat[1:], BF16), pltpu.VMEM(flat[1:], BF16),
                pltpu.VMEM((layers, heads * hd, dm), BF16),
                pltpu.VMEM((layers, ny, dm, ffc), BF16),
                pltpu.VMEM((layers, ny, ffc, dm), BF16),
                pltpu.VMEM((layers, rloc, seq * heads, hd), BF16),
                pltpu.VMEM((layers, rloc, seq * heads, hd), BF16),
                pltpu.VMEM((layers, seq, heads, hd), BF16),
                pltpu.VMEM((2 * seq, heads, hd), BF16),
                pltpu.VMEM((ns, srow, dm), BF16),
                pltpu.VMEM((ny * grp, dm), BF16),
                pltpu.VMEM((128, 128 * heads), BF16),
                pltpu.VMEM((ny * grp, dm * heads), BF16),
                pltpu.VMEM((ns, 3, ny, grp, hd), BF16),
                pltpu.VMEM((layers, ns, 3, ny, grp, hd), BF16),
                pltpu.VMEM((layers, ns, 2, ny, 8, 128), F32),
                pltpu.VMEM((3, grp, hd), F32),
                pltpu.VMEM((ny * grp, hd), F32),
                pltpu.VMEM((layers, ns, ny, grp, hd), BF16),
                pltpu.VMEM((srow, heads * hd), BF16),
                pltpu.VMEM((layers, ns, 2, nx, srow, dm), BF16),
                pltpu.VMEM((ns, ny, srow, ffc), BF16),
                pltpu.VMEM((layers, ns, ny, srow, ffc), BF16),
                pltpu.VMEM((layers, ns, ny, srow, ffc), BF16),
                pltpu.VMEM((ns, srow, dm), F32),
                pltpu.SemaphoreType.DMA((layers, 7 + 2 * ny)),
                pltpu.SemaphoreType.DMA((layers, ns, nph, npeer)),
                pltpu.SemaphoreType.DMA((layers, ns, nph, npeer)),
            ],
            compiler_params=pltpu.CompilerParams(
                collective_id=0, has_side_effects=True, vmem_limit_bytes=67043328),
        )(hidden, lengths, k_cache.reshape(layers, rloc, seq * heads, hd), v_cache.reshape(layers, rloc, seq * heads, hd),
          rel_table, norm_attn, w_q.reshape(flat), w_k.reshape(flat), w_v.reshape(flat), bias_content, bias_pos,
          w_out.reshape(layers, heads * hd, dm), norm_mlp, w_up, w_down)
        nunit = 2 * layers * 2
        cache_shape = jax.ShapeDtypeStruct(k_cache.shape, BF16)
        return pl.pallas_call(
            write_kernel,
            name="write_caches",
            out_shape=(jax.ShapeDtypeStruct((rows, dm), BF16), cache_shape, cache_shape),
            in_specs=[vm, sm, vm, vm, hbm, hbm],
            out_specs=(vm, hbm, hbm),
            scratch_shapes=[
                pltpu.VMEM((nunit, rloc // 2, seq, heads, hd), BF16),
                pltpu.SemaphoreType.DMA((nunit,)),
                pltpu.SemaphoreType.DMA((nunit,)),
            ],
            compiler_params=pltpu.CompilerParams(vmem_limit_bytes=67043328),
        )(out, lengths, k_new, v_new, k_cache, v_cache)

    return jax.shard_map(local_step, mesh=mesh, in_specs=in_specs, out_specs=out_specs, check_vma=False)
```

time: 91.5 us -> 80.2 us (0.88)
  local copies, waits for them, and re-layouts: 7.38 us -> 0 us
  Pallas kernels: 83 us -> 79.3 us
    unnamed x12 -> x0, local copies, waits for them, and re-layouts: 7.38 us -> none
    pallas_call x1, Pallas kernels: 77.8 us -> 71.4 us  [local_step(): pl.pallas_call(functools.partial(layers_kernel, ny, nx, ns), name='decode...]
    pallas_call x1, Pallas kernels: 5.19 us -> 7.93 us  [local_step(): pl.pallas_call(write_kernel, name='write_caches', out_shape=(jax.ShapeDty...]
where the time goes in v3:
time: 80.2 us; the launch traced here: 80 us
  Pallas kernels  79.3 us (99%)
    pallas_call x1, Pallas kernels, local_step(): pl.pallas_call(functools.partial(layers_kernel, ny, nx, ns), name='decode...  71.4 us
    pallas_call x1, Pallas kernels, local_step(): pl.pallas_call(write_kernel, name='write_caches', out_shape=(jax.ShapeDty...  7.93 us

profile of v3, /device:TPU:0, one launch (start us, length us, event | category | flops | bytes accessed | tf_op | source)
XLA Modules:
  0.0 80.0 jit_solution(10874920120032078359)
XLA Ops:
  0.6 71.4 %decode_layers.1 = (bf16[32,1024]{1,0:T(8,128)(2,1)}, bf16[2,8,8,128]{3,2,1,0:T(8,128)(2,1)}, bf16[2,8,8,128]{3,2,1,0:T(8,128)(2,1)}) custom-call(bf16[32,1024]{1,0:T(8,128)(2,1)} %x_ref.1, s32[32]{0:T(128)} %len_ref.3, bf16[2,8,1024,128]{3,2,1,0:T(8,128)(2,1)} %bitcast.6, bf16[2,8,1024,128]{3,2,1,0:T(8,128)(2,1)} %bitcast.7, ...), custom_call_target="tpu_custom_call" | custom-call | tf_op jit(solution)/shard_map/decode_layers/pallas_call | solution.py:388
  72.1 7.9 %write_caches.1 = (bf16[32,1024]{1,0:T(8,128)(2,1)}, bf16[2,8,128,8,128]{4,3,2,1,0:T(8,128)(2,1)}, bf16[2,8,128,8,128]{4,3,2,1,0:T(8,128)(2,1)}) custom-call(bf16[32,1024]{1,0:T(8,128)(2,1)} %get-tuple-element.6.x_ref, s32[32]{0:T(128)} %len_ref.3, bf16[2,8,8,128]{3,2,1,0:T(8,128)(2,1)} %get-tuple-element.7.kn_ref, ...), custom_call_target="tpu_custom_call" | custom-call | tf_op jit(solution)/shard_map/write_caches/pallas_call | solution.py:430

commit v4 on v3

--- a/solution.py
+++ b/solution.py
@@ -20,11 +20,12 @@
 
 def layers_kernel(
     ny, nx, ns,
-    x_ref, len_ref, k_hbm, v_hbm, rel_hbm, ga_ref, wq_hbm, wk_hbm, wv_hbm, u_ref, w_ref, wo_hbm, gm_ref, wup_hbm, wdn_hbm,
-    xout_ref, knew_ref, vnew_ref,
+    x_hbm, len_hbm, k_hbm, v_hbm, rel_hbm, ga_hbm, wq_hbm, wk_hbm, wv_hbm, u_hbm, w_hbm, wo_hbm, gm_hbm, wup_hbm, wdn_hbm,
+    out_ref,
     wq, wk, wv, wo, wup, wdn, kbuf, vbuf, rel, relrev,
+    x_ref, len_ref, ga_ref, u_ref, w_ref, gm_ref,
     xcur, hrep, expand, lhs, qkv_send, qkv_recv, stat, qkvf, ctxf, ctx_recv, lhs_wo, ar, up_send, up_recv, act, down,
-    wsem, send_sem, recv_sem,
+    ssem, wsem, send_sem, recv_sem,
 ):
     layers = wup_hbm.shape[0]
     rows, dm = x_ref.shape
@@ -37,6 +38,7 @@
     nblk = dm // 128
     wide = 128 * heads
     grp = heads * sloc
+    nxt = nblk * rows // 8
     r = lax.axis_index("rep")
     y = lax.axis_index("y")
     x = lax.axis_index("x")
@@ -49,17 +51,20 @@
         return [pltpu.make_async_copy(s, d, wsem.at[l, i]) for i, (s, d) in enumerate(pairs)]
 
     def load_rest(l):
-        out = [(k_hbm.at[l], kbuf.at[l]), (rel_hbm.at[l], rel.at[l]), (v_hbm.at[l], vbuf.at[l]), (wo_hbm.at[l], wo.at[l])]
+        out = [(k_hbm.at[l], kbuf), (rel_hbm.at[l], rel.at[l]), (v_hbm.at[l], vbuf), (wo_hbm.at[l], wo.at[l])]
         for c in range(ny):
             out.append((wup_hbm.at[l, :, pl.ds(c * ffc, ffc)], wup.at[l, c]))
         for c in range(ny):
             out.append((wdn_hbm.at[l, pl.ds(c * ffc, ffc), :], wdn.at[l, c]))
         return [pltpu.make_async_copy(s, d, wsem.at[l, 3 + i]) for i, (s, d) in enumerate(out)]
 
-    for c in load_qkv(0):
+    smalls = [pltpu.make_async_copy(a, b, ssem.at[i]) for i, (a, b) in enumerate(
+        ((x_hbm, x_ref), (ga_hbm, ga_ref), (len_hbm, len_ref), (u_hbm, u_ref), (w_hbm, w_ref), (gm_hbm, gm_ref)))]
+    for c in smalls[:2] + load_qkv(0) + smalls[2:] + load_rest(0):
         c.start()
-    for l in range(layers):
-        for c in load_rest(l):
+    for l in range(1, layers):
+        rest = load_rest(l)
+        for c in rest[1:2] + rest[3:]:
             c.start()
 
     barrier = pltpu.get_barrier_semaphore()
@@ -67,6 +72,9 @@
         pl.semaphore_signal(barrier, inc=1, device_id=(r, py, x), device_id_type=MESH)
     for px in xpeers:
         pl.semaphore_signal(barrier, inc=1, device_id=(r, y, px), device_id_type=MESH)
+
+    for c in smalls:
+        c.wait()
 
     def iota(shape, dim):
         return lax.broadcasted_iota(jnp.int32, shape, dim)
@@ -90,8 +98,6 @@
     igrp = iota((grp, 128), 0) % sloc + sloc * y
     lgrp = iota((grp, 128), 1)
 
-    pl.semaphore_wait(barrier, (ny - 1) + (nx - 1))
-
     def copy_y(l, s, ph, src, dst, py):
         return pltpu.make_async_remote_copy(
             src_ref=src, dst_ref=dst, send_sem=send_sem.at[l, s, ph, py], recv_sem=recv_sem.at[l, s, ph, y],
@@ -119,9 +125,11 @@
         t = jnp.sum(xw * xw, axis=1, keepdims=True) * (1.0 / dm) + EPS
         t_row = jnp.sum(jnp.where(irow == lrow, jnp.broadcast_to(t, (srow, 128)), 0.0), axis=0, keepdims=True)
         stat[l, s, ph, y] = jnp.broadcast_to(t_row, (8, 128))
+        return (xw * lax.rsqrt(t) * gain).astype(BF16)
+
+    def stat_send(l, s, ph):
         for py in ypeers:
             copy_y(l, s, ph, stat.at[l, s, ph, y], stat.at[l, s, ph, y], py).start()
-        return (xw * lax.rsqrt(t) * gain).astype(BF16)
 
     def ratio_rows(l, s, ph):
         for py in ypeers:
@@ -147,18 +155,27 @@
 
     PQ, PC, PA, PD, PU, PG = 2, 5, 6, 7, 8, 9
 
-    def project(l, s, first):
+    kh = dm * heads // 2
+    kq = kh // 2
+    bh = nblk // 2
+    mg = ny * grp
+
+    def project(l, s, first, wait_barrier=False):
         wl = load_qkv(l)
         h = norm_local(l, s, 0, gain_row(ga_ref, l))
+        if not wait_barrier:
+            stat_send(l, s, 0)
         hrep[...] = dot(repeat, h).astype(BF16)
         for b in range(nblk):
             hx = dot(hrep[:, b * 128:(b + 1) * 128], expand[...])
-            lhs[:, b * wide:(b + 1) * wide] = jnp.where(own_head, hx if b < nblk // 2 else -hx, 0.0).astype(BF16)
-        kh = dm * heads // 2
-
-        def scatter(i, part):
+            r0, c0 = (b // bh) * mg, (b % bh) * wide
+            lhs[r0:r0 + mg, c0:c0 + wide] = jnp.where(own_head, hx if b < bh else -hx, 0.0).astype(BF16)
+
+        def put(i, part):
             for p in range(ny):
                 qkv_send[s, i, p] = part[p * grp:(p + 1) * grp, :].astype(BF16)
+
+        def scatter(i):
             for py in ypeers:
                 copy_y(l, s, PQ + i, qkv_send.at[s, i, py], qkv_recv.at[l, s, i, y], py).start()
             qkv_recv[l, s, i, y] = qkv_send[s, i, y]
@@ -166,13 +183,21 @@
         if first:
             wl[0].wait()
             wl[1].wait()
-        qk = (dot(lhs[:, :kh], jnp.concatenate([wq[:kh, :], wk[:kh, :]], axis=1))
-              - dot(lhs[:, kh:], jnp.concatenate([wq[kh:, :], wk[kh:, :]], axis=1)))
-        scatter(0, qk[:, :hd])
-        scatter(1, qk[:, hd:])
+        qk = (dot(lhs[:mg, :], jnp.concatenate([wq[:kh, :], wk[:kh, :]], axis=1))
+              - dot(lhs[mg:, :], jnp.concatenate([wq[kh:, :], wk[kh:, :]], axis=1)))
+        put(0, qk[:, :hd])
+        put(1, qk[:, hd:])
+        if wait_barrier:
+            pl.semaphore_wait(barrier, (ny - 1) + (nx - 1))
+            stat_send(l, s, 0)
+        scatter(0)
+        scatter(1)
         if first:
             wl[2].wait()
-        scatter(2, dot(lhs[:, :kh], wv[:kh, :]) - dot(lhs[:, kh:], wv[kh:, :]))
+        v1 = dot(lhs[:, :kq], jnp.concatenate([wv[:kq, :], wv[kh:kh + kq, :]], axis=1))
+        v2 = dot(lhs[:, kq:], jnp.concatenate([wv[kq:kh, :], wv[kh + kq:, :]], axis=1))
+        put(2, (v1[:mg, :hd] - v1[mg:, hd:]) + (v2[:mg, :hd] - v2[mg:, hd:]))
+        scatter(2)
 
     sub = iota((heads, seq * heads), 0)
     col = iota((heads, seq * heads), 1)
@@ -207,7 +232,7 @@
             a, cc = (q + ul).astype(BF16), (q + pl_bias).astype(BF16)
             queries.append((a, cc))
             window = relrev[pl.ds(seq - 1 - length, seq)].reshape(seq * heads, hd)
-            sc = lax.dot_general(a, kbuf[l, s * sloc + b], NT, preferred_element_type=F32)
+            sc = lax.dot_general(a, kbuf[s * sloc + b], NT, preferred_element_type=F32)
             sc = sc + lax.dot_general(cc, window, NT, preferred_element_type=F32)
             scores.append(jnp.where(own & (pos < length), sc * scale, -1e30))
         gather(1)
@@ -219,8 +244,8 @@
             sc = scores[b]
             k = qkvf[1, pl.ds(b, heads, stride=sloc), :]
             v = qkvf[2, pl.ds(b, heads, stride=sloc), :]
-            knew_ref[l, s * sloc + b] = k.astype(BF16)
-            vnew_ref[l, s * sloc + b] = v.astype(BF16)
+            out_ref[nxt + l * rloc + s * sloc + b] = k.astype(BF16)
+            out_ref[nxt + (layers + l) * rloc + s * sloc + b] = v.astype(BF16)
             sn = jnp.sum(a.astype(F32) * k + cc.astype(F32) * rel0, axis=1, keepdims=True) * scale
             m = jnp.maximum(jnp.max(sc, axis=1, keepdims=True), sn)
             e = jnp.exp(sc - m)
@@ -228,7 +253,7 @@
             z = jnp.sum(e, axis=1, keepdims=True) + en
             pr = (e / z).astype(BF16)
             pn = (en / z).astype(BF16).astype(F32)
-            ctxf[b * heads:(b + 1) * heads, :] = dot(pr, vbuf[l, s * sloc + b]) + pn * v
+            ctxf[b * heads:(b + 1) * heads, :] = dot(pr, vbuf[s * sloc + b]) + pn * v
         ctx_recv[l, s, y] = ctxf[0:grp, :].astype(BF16)
         for py in ypeers:
             copy_y(l, s, PC, ctx_recv.at[l, s, y], ctx_recv.at[l, s, y], py).start()
@@ -248,6 +273,7 @@
     def ff_up(l, s, first):
         reduce_finish(l, s, PA, 0)
         h2 = norm_local(l, s, 1, gain_row(gm_ref, l))
+        stat_send(l, s, 1)
         if first:
             for c in load_rest(l)[4:4 + ny]:
                 c.wait()
@@ -291,21 +317,26 @@
 
     relrev[pl.ds(seq, seq)] = jnp.zeros((seq, heads, hd), BF16)
 
+    for s in range(ns):
+        project(0, s, s == 0, wait_barrier=s == 0)
+
     def layer(l, carry):
-        for s in range(ns):
-            @pl.when(l > 0)
-            def _():
-                reduce_finish(l - 1, s, PD, 1)
-
-            project(l, s, s == 0)
-
         @pl.when(l + 1 < layers)
         def _():
             for c in load_qkv(l + 1):
                 c.start()
 
         reverse_rel(l)
-        for stage in (attend, project_out, ff_up, ff_act, ff_down):
+        for s in range(ns):
+            attend(l, s, s == 0)
+
+        @pl.when(l + 1 < layers)
+        def _():
+            rest = load_rest(l + 1)
+            rest[0].start()
+            rest[2].start()
+
+        for stage in (project_out, ff_up, ff_act, ff_down):
             for s in range(ns):
                 stage(l, s, s == 0)
         for s in range(ns):
@@ -313,6 +344,13 @@
                 for i in range(3):
                     local(l, s, PQ + i, qkv_send.at[s, i, py], py).wait_send()
                 local(l, s, PU, up_send.at[s, py], py).wait_send()
+
+        @pl.when(l + 1 < layers)
+        def _():
+            for s in range(ns):
+                reduce_finish(l, s, PD, 1)
+                project(l + 1, s, s == 0)
+
         return carry
 
     lax.fori_loop(0, layers, layer, 0)
@@ -321,7 +359,8 @@
         reduce_finish(layers - 1, s, PD, 1)
         part = dot(ones_where(pick(s, (rows, srow), 1)), xcur[s])
         total = part if total is None else total + part
-    xout_ref[...] = total.astype(BF16)
+    for j in range(nblk):
+        out_ref[j * rows // 8:(j + 1) * rows // 8] = total[:, j * 128:(j + 1) * 128].astype(BF16).reshape(rows // 8, 8, 128)
 
     def drain(l, carry):
         for s in range(ns):
@@ -338,25 +377,30 @@
     lax.fori_loop(0, layers, drain, 0)
 
 
-def write_kernel(x_ref, len_ref, kn_ref, vn_ref, k_hbm, v_hbm, xout_ref, kout, vout, buf, in_sem, out_sem):
-    layers, rloc = kn_ref.shape[:2]
+def write_kernel(len_ref, new_hbm, k_ref, v_ref, xout_hbm, kout, vout, x_buf, new_ref, small_sem, bulk_sem, row_sem):
+    layers, rloc = k_ref.shape[:2]
+    rows, dm = x_buf.shape
+    nblk = dm // 128
     y = lax.axis_index("y")
-    units = [(s, n, o, l) for l in range(layers) for s, n, o in ((k_hbm, kn_ref, kout), (v_hbm, vn_ref, vout))]
-    nsplit = 2
-    per = rloc // nsplit
-    steps = [(s, n, o, l, q) for (s, n, o, l) in units for q in range(nsplit)]
-    ins = [pltpu.make_async_copy(s.at[l, q * per:(q + 1) * per], buf.at[i], in_sem.at[i]) for i, (s, n, o, l, q) in enumerate(steps)]
-    outs = [pltpu.make_async_copy(buf.at[i], o.at[l, q * per:(q + 1) * per], out_sem.at[i]) for i, (s, n, o, l, q) in enumerate(steps)]
-    for c in ins:
+    units = [(i, src, out, l, b) for l in range(layers) for i, (src, out) in enumerate(((k_ref, kout), (v_ref, vout))) for b in range(rloc)]
+    bulk = [pltpu.make_async_copy(src.at[l, b], out.at[l, b], bulk_sem.at[n]) for n, (i, src, out, l, b) in enumerate(units)]
+    late = [pltpu.make_async_copy(new_ref.at[nblk * rows // 8 + (i * layers + l) * rloc + b], out.at[l, b, len_ref[rloc * y + b]], row_sem.at[n])
+            for n, (i, src, out, l, b) in enumerate(units)]
+    news = pltpu.make_async_copy(new_hbm, new_ref, small_sem.at[0])
+    news.start()
+    for c in bulk:
         c.start()
-    xout_ref[...] = x_ref[...]
-    for i, (s, n, o, l, q) in enumerate(steps):
-        ins[i].wait()
-        for b in range(per):
-            buf[i, b, len_ref[rloc * y + q * per + b]] = n[l, q * per + b]
-        outs[i].start()
-    for c in outs:
+    news.wait()
+    for j in range(nblk):
+        x_buf[:, j * 128:(j + 1) * 128] = new_ref[j * rows // 8:(j + 1) * rows // 8].reshape(rows, 128)
+    xout = pltpu.make_async_copy(x_buf, xout_hbm, small_sem.at[1])
+    xout.start()
+    for c, n in zip(bulk, late):
         c.wait()
+        n.start()
+    for n in late:
+        n.wait()
+    xout.wait()
 
 
 def solution(mesh):
@@ -379,31 +423,34 @@
         vm = pl.BlockSpec(memory_space=pltpu.VMEM)
         sm = pl.BlockSpec(memory_space=pltpu.SMEM)
         hbm = pl.BlockSpec(memory_space=pl.ANY)
-        new_shape = jax.ShapeDtypeStruct((layers, rloc, heads, hd), BF16)
+        hbm_only = pl.BlockSpec(memory_space=pltpu.HBM)
+        new_shape = jax.ShapeDtypeStruct((dm // 128 * rows // 8 + 2 * layers * rloc, 8, 128), BF16)
         ns = 2
         srow = rows // ns
         grp = heads * (rloc // ns)
         nph = 10
         npeer = max(ny, nx)
-        out, k_new, v_new = pl.pallas_call(
+        out = pl.pallas_call(
             functools.partial(layers_kernel, ny, nx, ns),
             name="decode_layers",
-            out_shape=(jax.ShapeDtypeStruct((rows, dm), BF16), new_shape, new_shape),
-            in_specs=[vm, sm, hbm, hbm, hbm, vm, hbm, hbm, hbm, vm, vm, hbm, vm, hbm, hbm],
-            out_specs=(vm, vm, vm),
+            out_shape=new_shape,
+            in_specs=[hbm] * 15,
+            out_specs=vm,
             scratch_shapes=[
                 pltpu.VMEM(flat[1:], BF16), pltpu.VMEM(flat[1:], BF16), pltpu.VMEM(flat[1:], BF16),
                 pltpu.VMEM((layers, heads * hd, dm), BF16),
                 pltpu.VMEM((layers, ny, dm, ffc), BF16),
                 pltpu.VMEM((layers, ny, ffc, dm), BF16),
-                pltpu.VMEM((layers, rloc, seq * heads, hd), BF16),
-                pltpu.VMEM((layers, rloc, seq * heads, hd), BF16),
+                pltpu.VMEM((rloc, seq * heads, hd), BF16),
+                pltpu.VMEM((rloc, seq * heads, hd), BF16),
                 pltpu.VMEM((layers, seq, heads, hd), BF16),
                 pltpu.VMEM((2 * seq, heads, hd), BF16),
+                pltpu.VMEM((rows, dm), BF16), pltpu.SMEM(lengths.shape, jnp.int32), pltpu.VMEM(norm_attn.shape, BF16),
+                pltpu.VMEM(bias_content.shape, BF16), pltpu.VMEM(bias_pos.shape, BF16), pltpu.VMEM(norm_mlp.shape, BF16),
                 pltpu.VMEM((ns, srow, dm), BF16),
                 pltpu.VMEM((ny * grp, dm), BF16),
                 pltpu.VMEM((128, 128 * heads), BF16),
-                pltpu.VMEM((ny * grp, dm * heads), BF16),
+                pltpu.VMEM((2 * ny * grp, dm * heads // 2), BF16),
                 pltpu.VMEM((ns, 3, ny, grp, hd), BF16),
                 pltpu.VMEM((layers, ns, 3, ny, grp, hd), BF16),
                 pltpu.VMEM((layers, ns, 2, ny, 8, 128), F32),
@@ -416,29 +463,29 @@
                 pltpu.VMEM((layers, ns, ny, srow, ffc), BF16),
                 pltpu.VMEM((layers, ns, ny, srow, ffc), BF16),
                 pltpu.VMEM((ns, srow, dm), F32),
+                pltpu.SemaphoreType.DMA((6,)),
                 pltpu.SemaphoreType.DMA((layers, 7 + 2 * ny)),
                 pltpu.SemaphoreType.DMA((layers, ns, nph, npeer)),
                 pltpu.SemaphoreType.DMA((layers, ns, nph, npeer)),
             ],
             compiler_params=pltpu.CompilerParams(
-                collective_id=0, has_side_effects=True, vmem_limit_bytes=67043328),
+                collective_id=0, has_side_effects=True, vmem_limit_bytes=109 << 19),
         )(hidden, lengths, k_cache.reshape(layers, rloc, seq * heads, hd), v_cache.reshape(layers, rloc, seq * heads, hd),
           rel_table, norm_attn, w_q.reshape(flat), w_k.reshape(flat), w_v.reshape(flat), bias_content, bias_pos,
           w_out.reshape(layers, heads * hd, dm), norm_mlp, w_up, w_down)
-        nunit = 2 * layers * 2
+        nunit = 2 * layers * rloc
         cache_shape = jax.ShapeDtypeStruct(k_cache.shape, BF16)
         return pl.pallas_call(
             write_kernel,
             name="write_caches",
             out_shape=(jax.ShapeDtypeStruct((rows, dm), BF16), cache_shape, cache_shape),
-            in_specs=[vm, sm, vm, vm, hbm, hbm],
-            out_specs=(vm, hbm, hbm),
+            in_specs=[sm, hbm_only, vm, vm],
+            out_specs=(hbm, hbm, hbm),
             scratch_shapes=[
-                pltpu.VMEM((nunit, rloc // 2, seq, heads, hd), BF16),
-                pltpu.SemaphoreType.DMA((nunit,)),
-                pltpu.SemaphoreType.DMA((nunit,)),
+                pltpu.VMEM((rows, dm), BF16), pltpu.VMEM(new_shape.shape, BF16),
+                pltpu.SemaphoreType.DMA((2,)), pltpu.SemaphoreType.DMA((nunit,)), pltpu.SemaphoreType.DMA((nunit,)),
             ],
-            compiler_params=pltpu.CompilerParams(vmem_limit_bytes=67043328),
-        )(out, lengths, k_new, v_new, k_cache, v_cache)
+            compiler_params=pltpu.CompilerParams(vmem_limit_bytes=16777216),
+        )(lengths, out, k_cache, v_cache)
 
     return jax.shard_map(local_step, mesh=mesh, in_specs=in_specs, out_specs=out_specs, check_vma=False)

time: 80.2 us -> 90.7 us (1.13)
  Pallas kernels: 79.3 us -> 88.7 us
  local copies, waits for them, and re-layouts: 0 us -> 0.91 us
    pallas_call x1, Pallas kernels: 71.4 us -> 83.6 us  [local_step(): pl.pallas_call(functools.partial(layers_kernel, ny, nx, ns), name='decode...]
    pallas_call x1, Pallas kernels: 7.93 us -> 5.14 us  [local_step(): pl.pallas_call(write_kernel, name='write_caches', out_shape=(jax.ShapeDty...]
    unnamed x0 -> x8, local copies, waits for them, and re-layouts: none -> 0.91 us
where the time goes in v4:
time: 90.7 us; the launch traced here: 90.5 us
  Pallas kernels  88.7 us (98%)
  local copies, waits for them, and re-layouts  0.91 us (1%)
    pallas_call x1, Pallas kernels, local_step(): pl.pallas_call(functools.partial(layers_kernel, ny, nx, ns), name='decode...  83.6 us
    pallas_call x1, Pallas kernels, local_step(): pl.pallas_call(write_kernel, name='write_caches', out_shape=(jax.ShapeDty...  5.14 us

profile of v4, /device:TPU:0, one launch (start us, length us, event | category | flops | bytes accessed | tf_op | source)
XLA Modules:
  0.0 90.5 jit_solution(7939908084270590994)
XLA Ops:
  0.6 0.0 copy-start
  0.6 0.0 copy-start.1
  0.7 0.0 copy-start.3
  0.7 83.6 %decode_layers.1.new_hbm = bf16[64,8,128]{2,1,0:T(8,128)(2,1)} custom-call(bf16[32,1024]{1,0:T(8,128)(2,1)} %x_hbm.1, s32[32]{0:T(128)} %len_ref.1, bf16[2,8,1024,128]{3,2,1,0:T(8,128)(2,1)} %bitcast.6, bf16[2,8,1024,128]{3,2,1,0:T(8,128)(2,1)} %bitcast.7, bf16[2,128,8,128]{3,2,1,0:T(8,128)(2,1)} %rel_hbm.1, bf16[2,1024]{1,0:T(2,128)(2,1)} %ga_hbm.1, ...), custom_call_target="tpu_custom_call" | custom-call | tf_op jit(solution)/shard_map/decode_layers/pallas_call | solution.py:433
  84.3 0.0 copy-done
  84.3 0.0 copy-done.1
  84.3 0.0 copy-done.3
  84.3 0.0 copy-start.2
  84.3 0.9 copy-done.2
  85.2 5.1 %write_caches.1 = (bf16[32,1024]{1,0:T(8,128)(2,1)}, bf16[2,8,128,8,128]{4,3,2,1,0:T(8,128)(2,1)}, bf16[2,8,128,8,128]{4,3,2,1,0:T(8,128)(2,1)}) custom-call(s32[32]{0:T(128)S(1)} %copy-done.3, bf16[64,8,128]{2,1,0:T(8,128)(2,1)S(1)} %copy-done.2, bf16[2,8,128,8,128]{4,3,2,1,0:T(8,128)(2,1)S(1)} %copy-done, bf16[2,8,128,8,128]{4,3,2,1,0:T(8,128)(2,1)S(1)} %copy-done.1), custom_call_target="tpu_custom_call" | custom-call | tf_op jit(solution)/shard_map/write_caches/pallas_call | solution.py:478
Async XLA Ops:
  0.6 83.6 %copy-start = (bf16[2,8,128,8,128]{4,3,2,1,0:T(8,128)(2,1)S(1)}, bf16[2,8,128,8,128]{4,3,2,1,0:T(8,128)(2,1)}, u32[]{:S(2)}) copy-start(bf16[2,8,128,8,128]{4,3,2,1,0:T(8,128)(2,1)} %k_ref.1) | copy-start | bytes 12582916
  0.6 83.6 %copy-start.1 = (bf16[2,8,128,8,128]{4,3,2,1,0:T(8,128)(2,1)S(1)}, bf16[2,8,128,8,128]{4,3,2,1,0:T(8,128)(2,1)}, u32[]{:S(2)}) copy-start(bf16[2,8,128,8,128]{4,3,2,1,0:T(8,128)(2,1)} %v_ref.1) | copy-start | bytes 12582916
  0.7 83.6 %copy-start.3 = (s32[32]{0:T(128)S(1)}, s32[32]{0:T(128)}, u32[]{:S(2)}) copy-start(s32[32]{0:T(128)} %len_ref.1) | copy-start | bytes 388
  84.3 0.9 %copy-start.2 = (bf16[64,8,128]{2,1,0:T(8,128)(2,1)S(1)}, bf16[64,8,128]{2,1,0:T(8,128)(2,1)}, u32[]{:S(2)}) copy-start(bf16[64,8,128]{2,1,0:T(8,128)(2,1)} %decode_layers.1.new_hbm) | copy-start | bytes 393220

commit v5 on v3

--- a/solution.py
+++ b/solution.py
@@ -21,7 +21,7 @@
 def layers_kernel(
     ny, nx, ns,
     x_ref, len_ref, k_hbm, v_hbm, rel_hbm, ga_ref, wq_hbm, wk_hbm, wv_hbm, u_ref, w_ref, wo_hbm, gm_ref, wup_hbm, wdn_hbm,
-    xout_ref, knew_ref, vnew_ref,
+    out_ref,
     wq, wk, wv, wo, wup, wdn, kbuf, vbuf, rel, relrev,
     xcur, hrep, expand, lhs, qkv_send, qkv_recv, stat, qkvf, ctxf, ctx_recv, lhs_wo, ar, up_send, up_recv, act, down,
     wsem, send_sem, recv_sem,
@@ -37,6 +37,7 @@
     nblk = dm // 128
     wide = 128 * heads
     grp = heads * sloc
+    nxt = nblk * rows // 8
     r = lax.axis_index("rep")
     y = lax.axis_index("y")
     x = lax.axis_index("x")
@@ -147,18 +148,25 @@
 
     PQ, PC, PA, PD, PU, PG = 2, 5, 6, 7, 8, 9
 
+    kh = dm * heads // 2
+    kq = kh // 2
+    bh = nblk // 2
+    mg = ny * grp
+
     def project(l, s, first):
         wl = load_qkv(l)
         h = norm_local(l, s, 0, gain_row(ga_ref, l))
         hrep[...] = dot(repeat, h).astype(BF16)
         for b in range(nblk):
             hx = dot(hrep[:, b * 128:(b + 1) * 128], expand[...])
-            lhs[:, b * wide:(b + 1) * wide] = jnp.where(own_head, hx if b < nblk // 2 else -hx, 0.0).astype(BF16)
-        kh = dm * heads // 2
-
-        def scatter(i, part):
+            r0, c0 = (b // bh) * mg, (b % bh) * wide
+            lhs[r0:r0 + mg, c0:c0 + wide] = jnp.where(own_head, hx if b < bh else -hx, 0.0).astype(BF16)
+
+        def put(i, part):
             for p in range(ny):
                 qkv_send[s, i, p] = part[p * grp:(p + 1) * grp, :].astype(BF16)
+
+        def scatter(i):
             for py in ypeers:
                 copy_y(l, s, PQ + i, qkv_send.at[s, i, py], qkv_recv.at[l, s, i, y], py).start()
             qkv_recv[l, s, i, y] = qkv_send[s, i, y]
@@ -166,13 +174,18 @@
         if first:
             wl[0].wait()
             wl[1].wait()
-        qk = (dot(lhs[:, :kh], jnp.concatenate([wq[:kh, :], wk[:kh, :]], axis=1))
-              - dot(lhs[:, kh:], jnp.concatenate([wq[kh:, :], wk[kh:, :]], axis=1)))
-        scatter(0, qk[:, :hd])
-        scatter(1, qk[:, hd:])
+        qk = (dot(lhs[:mg, :], jnp.concatenate([wq[:kh, :], wk[:kh, :]], axis=1))
+              - dot(lhs[mg:, :], jnp.concatenate([wq[kh:, :], wk[kh:, :]], axis=1)))
+        put(0, qk[:, :hd])
+        put(1, qk[:, hd:])
+        scatter(0)
+        scatter(1)
         if first:
             wl[2].wait()
-        scatter(2, dot(lhs[:, :kh], wv[:kh, :]) - dot(lhs[:, kh:], wv[kh:, :]))
+        v1 = dot(lhs[:, :kq], jnp.concatenate([wv[:kq, :], wv[kh:kh + kq, :]], axis=1))
+        v2 = dot(lhs[:, kq:], jnp.concatenate([wv[kq:kh, :], wv[kh + kq:, :]], axis=1))
+        put(2, (v1[:mg, :hd] - v1[mg:, hd:]) + (v2[:mg, :hd] - v2[mg:, hd:]))
+        scatter(2)
 
     sub = iota((heads, seq * heads), 0)
     col = iota((heads, seq * heads), 1)
@@ -219,8 +232,8 @@
             sc = scores[b]
             k = qkvf[1, pl.ds(b, heads, stride=sloc), :]
             v = qkvf[2, pl.ds(b, heads, stride=sloc), :]
-            knew_ref[l, s * sloc + b] = k.astype(BF16)
-            vnew_ref[l, s * sloc + b] = v.astype(BF16)
+            out_ref[nxt + l * rloc + s * sloc + b] = k.astype(BF16)
+            out_ref[nxt + (layers + l) * rloc + s * sloc + b] = v.astype(BF16)
             sn = jnp.sum(a.astype(F32) * k + cc.astype(F32) * rel0, axis=1, keepdims=True) * scale
             m = jnp.maximum(jnp.max(sc, axis=1, keepdims=True), sn)
             e = jnp.exp(sc - m)
@@ -321,7 +334,8 @@
         reduce_finish(layers - 1, s, PD, 1)
         part = dot(ones_where(pick(s, (rows, srow), 1)), xcur[s])
         total = part if total is None else total + part
-    xout_ref[...] = total.astype(BF16)
+    for j in range(nblk):
+        out_ref[j * rows // 8:(j + 1) * rows // 8] = total[:, j * 128:(j + 1) * 128].astype(BF16).reshape(rows // 8, 8, 128)
 
     def drain(l, carry):
         for s in range(ns):
@@ -338,25 +352,33 @@
     lax.fori_loop(0, layers, drain, 0)
 
 
-def write_kernel(x_ref, len_ref, kn_ref, vn_ref, k_hbm, v_hbm, xout_ref, kout, vout, buf, in_sem, out_sem):
-    layers, rloc = kn_ref.shape[:2]
+def write_kernel(len_hbm, new_hbm, k_hbm, v_hbm, xout_hbm, kout, vout, len_ref, x_buf, new_ref, buf, small_sem, in_sem, out_sem):
+    layers, rloc = k_hbm.shape[:2]
+    rows, dm = x_buf.shape
+    nblk = dm // 128
+    per = buf.shape[1]
     y = lax.axis_index("y")
-    units = [(s, n, o, l) for l in range(layers) for s, n, o in ((k_hbm, kn_ref, kout), (v_hbm, vn_ref, vout))]
-    nsplit = 2
-    per = rloc // nsplit
-    steps = [(s, n, o, l, q) for (s, n, o, l) in units for q in range(nsplit)]
-    ins = [pltpu.make_async_copy(s.at[l, q * per:(q + 1) * per], buf.at[i], in_sem.at[i]) for i, (s, n, o, l, q) in enumerate(steps)]
-    outs = [pltpu.make_async_copy(buf.at[i], o.at[l, q * per:(q + 1) * per], out_sem.at[i]) for i, (s, n, o, l, q) in enumerate(steps)]
-    for c in ins:
+    units = [(i, src, out, l, q * per) for l in range(layers) for i, (src, out) in enumerate(((k_hbm, kout), (v_hbm, vout)))
+             for q in range(rloc // per)]
+    smalls = [pltpu.make_async_copy(len_hbm, len_ref, small_sem.at[0]), pltpu.make_async_copy(new_hbm, new_ref, small_sem.at[1])]
+    ins = [pltpu.make_async_copy(src.at[l, pl.ds(q, per)], buf.at[n], in_sem.at[n]) for n, (i, src, out, l, q) in enumerate(units)]
+    outs = [pltpu.make_async_copy(buf.at[n], out.at[l, pl.ds(q, per)], out_sem.at[n]) for n, (i, src, out, l, q) in enumerate(units)]
+    for c in smalls + ins:
         c.start()
-    xout_ref[...] = x_ref[...]
-    for i, (s, n, o, l, q) in enumerate(steps):
-        ins[i].wait()
+    for c in smalls:
+        c.wait()
+    for j in range(nblk):
+        x_buf[:, j * 128:(j + 1) * 128] = new_ref[j * rows // 8:(j + 1) * rows // 8].reshape(rows, 128)
+    xout = pltpu.make_async_copy(x_buf, xout_hbm, small_sem.at[2])
+    xout.start()
+    for n, (i, src, out, l, q) in enumerate(units):
+        ins[n].wait()
         for b in range(per):
-            buf[i, b, len_ref[rloc * y + q * per + b]] = n[l, q * per + b]
-        outs[i].start()
+            buf[n, b, len_ref[rloc * y + q + b]] = new_ref[nblk * rows // 8 + (i * layers + l) * rloc + q + b]
+        outs[n].start()
     for c in outs:
         c.wait()
+    xout.wait()
 
 
 def solution(mesh):
@@ -379,18 +401,18 @@
         vm = pl.BlockSpec(memory_space=pltpu.VMEM)
         sm = pl.BlockSpec(memory_space=pltpu.SMEM)
         hbm = pl.BlockSpec(memory_space=pl.ANY)
-        new_shape = jax.ShapeDtypeStruct((layers, rloc, heads, hd), BF16)
+        new_shape = jax.ShapeDtypeStruct((dm // 128 * rows // 8 + 2 * layers * rloc, 8, 128), BF16)
         ns = 2
         srow = rows // ns
         grp = heads * (rloc // ns)
         nph = 10
         npeer = max(ny, nx)
-        out, k_new, v_new = pl.pallas_call(
+        out = pl.pallas_call(
             functools.partial(layers_kernel, ny, nx, ns),
             name="decode_layers",
-            out_shape=(jax.ShapeDtypeStruct((rows, dm), BF16), new_shape, new_shape),
+            out_shape=new_shape,
             in_specs=[vm, sm, hbm, hbm, hbm, vm, hbm, hbm, hbm, vm, vm, hbm, vm, hbm, hbm],
-            out_specs=(vm, vm, vm),
+            out_specs=vm,
             scratch_shapes=[
                 pltpu.VMEM(flat[1:], BF16), pltpu.VMEM(flat[1:], BF16), pltpu.VMEM(flat[1:], BF16),
                 pltpu.VMEM((layers, heads * hd, dm), BF16),
@@ -403,7 +425,7 @@
                 pltpu.VMEM((ns, srow, dm), BF16),
                 pltpu.VMEM((ny * grp, dm), BF16),
                 pltpu.VMEM((128, 128 * heads), BF16),
-                pltpu.VMEM((ny * grp, dm * heads), BF16),
+                pltpu.VMEM((2 * ny * grp, dm * heads // 2), BF16),
                 pltpu.VMEM((ns, 3, ny, grp, hd), BF16),
                 pltpu.VMEM((layers, ns, 3, ny, grp, hd), BF16),
                 pltpu.VMEM((layers, ns, 2, ny, 8, 128), F32),
@@ -425,20 +447,25 @@
         )(hidden, lengths, k_cache.reshape(layers, rloc, seq * heads, hd), v_cache.reshape(layers, rloc, seq * heads, hd),
           rel_table, norm_attn, w_q.reshape(flat), w_k.reshape(flat), w_v.reshape(flat), bias_content, bias_pos,
           w_out.reshape(layers, heads * hd, dm), norm_mlp, w_up, w_down)
-        nunit = 2 * layers * 2
+        per = 2
+        nunit = 2 * layers * (rloc // per)
         cache_shape = jax.ShapeDtypeStruct(k_cache.shape, BF16)
         return pl.pallas_call(
             write_kernel,
             name="write_caches",
             out_shape=(jax.ShapeDtypeStruct((rows, dm), BF16), cache_shape, cache_shape),
-            in_specs=[vm, sm, vm, vm, hbm, hbm],
-            out_specs=(vm, hbm, hbm),
+            in_specs=[hbm] * 4,
+            out_specs=(hbm, hbm, hbm),
             scratch_shapes=[
-                pltpu.VMEM((nunit, rloc // 2, seq, heads, hd), BF16),
+                pltpu.SMEM(lengths.shape, jnp.int32),
+                pltpu.VMEM((rows, dm), BF16),
+                pltpu.VMEM(new_shape.shape, BF16),
+                pltpu.VMEM((nunit, per, seq, heads, hd), BF16),
+                pltpu.SemaphoreType.DMA((3,)),
                 pltpu.SemaphoreType.DMA((nunit,)),
                 pltpu.SemaphoreType.DMA((nunit,)),
             ],
             compiler_params=pltpu.CompilerParams(vmem_limit_bytes=67043328),
-        )(out, lengths, k_new, v_new, k_cache, v_cache)
+        )(lengths, out, k_cache, v_cache)
 
     return jax.shard_map(local_step, mesh=mesh, in_specs=in_specs, out_specs=out_specs, check_vma=False)

time: 80.2 us -> 78.6 us (0.980)
  Pallas kernels: 79.3 us -> 77.8 us
    pallas_call x1, Pallas kernels: 7.93 us -> 6.85 us  [local_step(): pl.pallas_call(write_kernel, name='write_caches', out_shape=(jax.ShapeDty...]
where the time goes in v5:
time: 78.6 us; the launch traced here: 78.4 us
  Pallas kernels  77.8 us (99%)
    pallas_call x1, Pallas kernels, local_step(): pl.pallas_call(functools.partial(layers_kernel, ny, nx, ns), name='decode...  70.9 us
    pallas_call x1, Pallas kernels, local_step(): pl.pallas_call(write_kernel, name='write_caches', out_shape=(jax.ShapeDty...  6.85 us

profile of v5, /device:TPU:0, one launch (start us, length us, event | category | flops | bytes accessed | tf_op | source)
XLA Modules:
  0.0 78.4 jit_solution(11843247719190282301)
XLA Ops:
  0.6 70.9 %decode_layers.1.new_hbm = bf16[64,8,128]{2,1,0:T(8,128)(2,1)} custom-call(bf16[32,1024]{1,0:T(8,128)(2,1)} %x_ref.1, s32[32]{0:T(128)} %len_hbm.1, bf16[2,8,1024,128]{3,2,1,0:T(8,128)(2,1)} %bitcast.6, bf16[2,8,1024,128]{3,2,1,0:T(8,128)(2,1)} %bitcast.7, bf16[2,128,8,128]{3,2,1,0:T(8,128)(2,1)} %rel_hbm.1, bf16[2,1024]{1,0:T(2,128)(2,1)} %ga_ref.1, ...), custom_call_target="tpu_custom_call" | custom-call | tf_op jit(solution)/shard_map/decode_layers/pallas_call | solution.py:410
  71.6 6.9 %write_caches.1 = (bf16[32,1024]{1,0:T(8,128)(2,1)}, bf16[2,8,128,8,128]{4,3,2,1,0:T(8,128)(2,1)}, bf16[2,8,128,8,128]{4,3,2,1,0:T(8,128)(2,1)}) custom-call(s32[32]{0:T(128)} %len_hbm.1, bf16[64,8,128]{2,1,0:T(8,128)(2,1)} %decode_layers.1.new_hbm, bf16[2,8,128,8,128]{4,3,2,1,0:T(8,128)(2,1)} %k_hbm.1, bf16[2,8,128,8,128]{4,3,2,1,0:T(8,128)(2,1)} %v_hbm.1), custom_call_target="tpu_custom_call" | custom-call | tf_op jit(solution)/shard_map/write_caches/pallas_call | solution.py:453

commit v6 on v5

--- a/solution.py
+++ b/solution.py
@@ -91,8 +91,6 @@
     igrp = iota((grp, 128), 0) % sloc + sloc * y
     lgrp = iota((grp, 128), 1)
 
-    pl.semaphore_wait(barrier, (ny - 1) + (nx - 1))
-
     def copy_y(l, s, ph, src, dst, py):
         return pltpu.make_async_remote_copy(
             src_ref=src, dst_ref=dst, send_sem=send_sem.at[l, s, ph, py], recv_sem=recv_sem.at[l, s, ph, y],
@@ -120,9 +118,11 @@
         t = jnp.sum(xw * xw, axis=1, keepdims=True) * (1.0 / dm) + EPS
         t_row = jnp.sum(jnp.where(irow == lrow, jnp.broadcast_to(t, (srow, 128)), 0.0), axis=0, keepdims=True)
         stat[l, s, ph, y] = jnp.broadcast_to(t_row, (8, 128))
+        return (xw * lax.rsqrt(t) * gain).astype(BF16)
+
+    def stat_send(l, s, ph):
         for py in ypeers:
             copy_y(l, s, ph, stat.at[l, s, ph, y], stat.at[l, s, ph, y], py).start()
-        return (xw * lax.rsqrt(t) * gain).astype(BF16)
 
     def ratio_rows(l, s, ph):
         for py in ypeers:
@@ -153,9 +153,11 @@
     bh = nblk // 2
     mg = ny * grp
 
-    def project(l, s, first):
+    def project(l, s, first, wait_barrier=False):
         wl = load_qkv(l)
         h = norm_local(l, s, 0, gain_row(ga_ref, l))
+        if not wait_barrier:
+            stat_send(l, s, 0)
         hrep[...] = dot(repeat, h).astype(BF16)
         for b in range(nblk):
             hx = dot(hrep[:, b * 128:(b + 1) * 128], expand[...])
@@ -178,6 +180,9 @@
               - dot(lhs[mg:, :], jnp.concatenate([wq[kh:, :], wk[kh:, :]], axis=1)))
         put(0, qk[:, :hd])
         put(1, qk[:, hd:])
+        if wait_barrier:
+            pl.semaphore_wait(barrier, (ny - 1) + (nx - 1))
+            stat_send(l, s, 0)
         scatter(0)
         scatter(1)
         if first:
@@ -261,6 +266,7 @@
     def ff_up(l, s, first):
         reduce_finish(l, s, PA, 0)
         h2 = norm_local(l, s, 1, gain_row(gm_ref, l))
+        stat_send(l, s, 1)
         if first:
             for c in load_rest(l)[4:4 + ny]:
                 c.wait()
@@ -304,21 +310,20 @@
 
     relrev[pl.ds(seq, seq)] = jnp.zeros((seq, heads, hd), BF16)
 
+    for s in range(ns):
+        project(0, s, s == 0, wait_barrier=s == 0)
+
     def layer(l, carry):
-        for s in range(ns):
-            @pl.when(l > 0)
-            def _():
-                reduce_finish(l - 1, s, PD, 1)
-
-            project(l, s, s == 0)
-
         @pl.when(l + 1 < layers)
         def _():
             for c in load_qkv(l + 1):
                 c.start()
 
         reverse_rel(l)
-        for stage in (attend, project_out, ff_up, ff_act, ff_down):
+        for s in range(ns):
+            attend(l, s, s == 0)
+
+        for stage in (project_out, ff_up, ff_act, ff_down):
             for s in range(ns):
                 stage(l, s, s == 0)
         for s in range(ns):
@@ -326,6 +331,13 @@
                 for i in range(3):
                     local(l, s, PQ + i, qkv_send.at[s, i, py], py).wait_send()
                 local(l, s, PU, up_send.at[s, py], py).wait_send()
+
+        @pl.when(l + 1 < layers)
+        def _():
+            for s in range(ns):
+                reduce_finish(l, s, PD, 1)
+                project(l + 1, s, s == 0)
+
         return carry
 
     lax.fori_loop(0, layers, layer, 0)

time: 78.6 us -> 79.2 us (level)
  no operation moved by 1% of the time
where the time goes in v6:
time: 79.2 us; the launch traced here: 79.1 us
  Pallas kernels  78.3 us (99%)
  between operations  0.8 us (1%)
    pallas_call x1, Pallas kernels, local_step(): pl.pallas_call(functools.partial(layers_kernel, ny, nx, ns), name='decode...  71.4 us
    pallas_call x1, Pallas kernels, local_step(): pl.pallas_call(write_kernel, name='write_caches', out_shape=(jax.ShapeDty...  6.85 us

profile of v6, /device:TPU:0, one launch (start us, length us, event | category | flops | bytes accessed | tf_op | source)
XLA Modules:
  0.0 79.1 jit_solution(16227681047085038648)
XLA Ops:
  0.6 71.4 %decode_layers.1.new_hbm = bf16[64,8,128]{2,1,0:T(8,128)(2,1)} custom-call(bf16[32,1024]{1,0:T(8,128)(2,1)} %x_ref.1, s32[32]{0:T(128)} %len_hbm.1, bf16[2,8,1024,128]{3,2,1,0:T(8,128)(2,1)} %bitcast.6, bf16[2,8,1024,128]{3,2,1,0:T(8,128)(2,1)} %bitcast.7, bf16[2,128,8,128]{3,2,1,0:T(8,128)(2,1)} %rel_hbm.1, bf16[2,1024]{1,0:T(2,128)(2,1)} %ga_ref.1, ...), custom_call_target="tpu_custom_call" | custom-call | tf_op jit(solution)/shard_map/decode_layers/pallas_call | solution.py:422
  72.0 6.9 %write_caches.1 = (bf16[32,1024]{1,0:T(8,128)(2,1)}, bf16[2,8,128,8,128]{4,3,2,1,0:T(8,128)(2,1)}, bf16[2,8,128,8,128]{4,3,2,1,0:T(8,128)(2,1)}) custom-call(s32[32]{0:T(128)} %len_hbm.1, bf16[64,8,128]{2,1,0:T(8,128)(2,1)} %decode_layers.1.new_hbm, bf16[2,8,128,8,128]{4,3,2,1,0:T(8,128)(2,1)} %k_hbm.1, bf16[2,8,128,8,128]{4,3,2,1,0:T(8,128)(2,1)} %v_hbm.1), custom_call_target="tpu_custom_call" | custom-call | tf_op jit(solution)/shard_map/write_caches/pallas_call | solution.py:465
